TPU v7x, 32 devices: a whole 2x2x4 slice. The times are simulated.
32 devices in a mesh: gx: 4 (over y, x), gy: 4 (over z), gz: 2 (over core).
Axes of the slice: x: 2, y: 2, z: 4, core: 2. Of those that a mesh axis runs over, the one named last changes fastest.
Arguments:
- ref_image: bfloat16 [1024, 64, 256], P('gx', 'gy', 'gz'), may hold values from -6 to 6
- def_image: bfloat16 [1024, 64, 256], P('gx', 'gy', 'gz'), may hold values from -6 to 6
- displacement: float32 [3, 128, 8, 32], P(None, 'gx', 'gy', 'gz'), may hold values from -3 to 3
Outputs:
- new_displacement: float32 [3, 128, 8, 32], P(None, 'gx', 'gy', 'gz')
- fine_residual: bfloat16 [1024, 64, 256], P('gx', 'gy', 'gz')
All inputs are finite; a program needn't handle non-finite values.
Results may differ from a plain program's by a relative error of at most 0.0022.
Values may be sent and summed in bfloat16 or wider, within the bound.
A program may use at most 64 MiB of HBM per device.

v0:
```python
import functools

import jax
import jax.numpy as jnp
import numpy as np
from jax import lax
from jax.experimental import pallas as pl
from jax.experimental.pallas import tpu as pltpu
from jax.sharding import PartitionSpec as P

stiffness = 64.0
BIN = 8
SLOT = 32
MESH = pl.DeviceIdType.MESH
HIGHEST = lax.Precision.HIGHEST


def inverse_table(devices, cells):
    lines = devices * cells
    theta = np.arccosh((1.0 + 2.0 * stiffness) / (2.0 * stiffness))
    index = np.arange(lines)
    low = np.minimum(index[:, None], index[None, :])
    high = np.maximum(index[:, None], index[None, :])
    a, b, c = (low + 1) * theta, (lines - high) * theta, (lines + 1) * theta
    inverse = (
        np.exp(a + b - c) * (1 - np.exp(-2 * a)) * (1 - np.exp(-2 * b)) / (1 - np.exp(-2 * c))
        / (2.0 * stiffness * np.sinh(theta))
    )
    table = np.zeros((devices, 3, cells + 16, cells + 8 * devices))
    sums = np.zeros((devices, 8, 3 * cells))
    for me in range(devices):
        first, last = me * cells, (me + 1) * cells - 1
        own = index[first : last + 1]
        up = np.exp((own - last) * theta) * (1 - np.exp(-2 * (own + 1) * theta)) / (1 - np.exp(-2 * (last + 1) * theta))
        down = (
            np.exp((first - own) * theta)
            * (1 - np.exp(-2 * (lines - own) * theta))
            / (1 - np.exp(-2 * (lines - first) * theta))
        )
        for k in range(3):
            sums[me, 2 * k, k * cells : (k + 1) * cells] = up
            sums[me, 2 * k + 1, k * cells : (k + 1) * cells] = down
            for row in range(7, cells + 9):
                x = first + row - 8
                if x < 0 or x >= lines:
                    continue
                table[me, k, row, :cells] = inverse[x, first : last + 1]
                for peer in range(devices):
                    if peer < me:
                        table[me, k, row, cells + 8 * peer + 2 * k] = inverse[x, (peer + 1) * cells - 1]
                    if peer > me:
                        table[me, k, row, cells + 8 * peer + 2 * k + 1] = inverse[x, peer * cells]
    return table.astype(np.float32), sums.astype(np.float32)


def lane_tables(cells_z, size_z, slots):
    place = np.zeros((cells_z, 3 * 128), np.float32)
    for variant in range(3):
        for z in range(cells_z):
            lane = z + 2 - (variant - 1) * cells_z
            if 0 <= lane < cells_z + 4:
                place[z, variant * 128 + lane] = 1.0
    binning = np.repeat(place, BIN, axis=0) / 32.0
    prolong = np.zeros((128, slots * size_z), np.float32)
    for slot in range(slots):
        for fine in range(size_z):
            lane, offset = slot * SLOT + fine // BIN + 2, (fine % BIN + 0.5) / BIN - 0.5
            prolong[lane, slot * size_z + fine] = 1.0 - abs(offset)
            prolong[lane + (1 if offset >= 0 else -1), slot * size_z + fine] = abs(offset)
    return place, binning, prolong


def exchange(
    counts,
    ref_hbm, def_hbm, disp_hbm, table_hbm, sums_hbm, place_hbm, bin_hbm, prolong_hbm,
    new_ref, lines, framed, def_ref, yout, zhalo,
    disp_ref, table_ref, sums_ref, place_ref, bin_ref, prolong_ref,
    binned, packed, halo, mine, theirs, xhalo, yrows, ysend, yhalo,
    load_sem,
    near_send, near_recv, peer_send, peer_recv, x_send, x_recv, y_send, y_recv, z_send, z_recv,
):
    nx, ny, nz = counts
    sizex, sizey, sizez = def_ref.shape
    ref_ref = framed.at[pl.ds(1, sizex)]
    cells_x, cells_z = sizex // BIN, sizez // BIN
    me = (lax.axis_index("gx"), lax.axis_index("gy"), lax.axis_index("gz"))

    def inside(offset):
        good = None
        for at, step, count in zip(me, offset, counts):
            if step:
                test = at > 0 if step < 0 else at < count - 1
                good = test if good is None else jnp.logical_and(good, test)
        return good

    def device(offset):
        return {"gx": me[0] + offset[0], "gy": me[1] + offset[1], "gz": me[2] + offset[2]}

    def peer(j):
        return {"gx": lax.rem(me[0] + j, nx), "gy": me[1], "gz": me[2]}

    steps = (-1, 0, 1)
    offsets = [(i, j, k) for i in steps for j in steps for k in steps if (i, j, k) != (0, 0, 0)]

    loads = [
        pltpu.make_async_copy(hbm, held, load_sem.at[i])
        for i, (hbm, held) in enumerate(
            (
                (disp_hbm, disp_ref), (place_hbm, place_ref), (ref_hbm, ref_ref), (def_hbm, def_ref),
                (bin_hbm, bin_ref), (sums_hbm.at[me[0]], sums_ref),
                (table_hbm.at[me[0]], table_ref), (prolong_hbm, prolong_ref),
            )
        )
    ]
    for load in loads:
        load.start()
    halo[...] = jnp.zeros_like(halo)
    theirs[...] = jnp.zeros_like(theirs)
    xhalo[...] = jnp.zeros_like(xhalo)
    yhalo[...] = jnp.zeros_like(yhalo)

    z_steps = (1,) if nz == 2 else (1, nz - 1)

    def z_device(step):
        return {"gx": me[0], "gy": me[1], "gz": lax.rem(me[2] + step, nz)}

    barrier = pltpu.get_barrier_semaphore()
    for j in range(1, nx):
        pl.semaphore_signal(barrier, inc=1, device_id=peer(j), device_id_type=MESH)
    expect = jnp.int32(nx - 1)
    for offset in offsets:
        if offset[1:] == (0, 0):
            continue

        @pl.when(inside(offset))
        def _():
            pl.semaphore_signal(barrier, inc=1, device_id=device(offset), device_id_type=MESH)

    reach = [
        1 + (at > 0).astype(jnp.int32) + (at < count - 1).astype(jnp.int32)
        for at, count in zip(me, counts)
    ]
    expect = expect + reach[0] * (reach[1] * reach[2] - 1)
    if nz > 2:
        ends = jnp.logical_or(me[2] == 0, me[2] == nz - 1)

        @pl.when(ends)
        def _():
            other = {"gx": me[0], "gy": me[1], "gz": nz - 1 - me[2]}
            pl.semaphore_signal(barrier, inc=1, device_id=other, device_id_type=MESH)

        expect = expect + ends.astype(jnp.int32)
    z_copies = [
        pltpu.make_async_remote_copy(
            src_ref=ref_ref, dst_ref=zhalo.at[i], send_sem=z_send.at[i], recv_sem=z_recv.at[i],
            device_id=z_device(step), device_id_type=MESH,
        )
        for i, step in enumerate(z_steps)
    ]

    source_rows = {-1: (0, 8), 0: (0, cells_x), 1: (cells_x - 8, 8)}
    target_rows = {-1: (0, 8), 0: (8, cells_x), 1: (cells_x + 8, 8)}

    def number(offset):
        return (offset[0] + 1) * 9 + (offset[1] + 1) * 3 + offset[2] + 1

    def blocks_of(step, part):
        return pl.ds(0, 1) if part == 0 else {-1: pl.ds(1, 1), 0: pl.ds(1, 2), 1: pl.ds(2, 1)}[step]

    def near_copy(offset, part):
        blocks = blocks_of(offset[1], part)
        back = tuple(-step for step in offset)
        start, rows = source_rows[offset[0]]
        goal = target_rows[back[0]][0]
        return pltpu.make_async_remote_copy(
            src_ref=packed.at[offset[2] + 1, blocks, pl.ds(start, rows), :],
            dst_ref=halo.at[back[1] + 1, back[2] + 1, blocks, pl.ds(goal, rows), :],
            send_sem=near_send.at[number(offset), part],
            recv_sem=near_recv.at[number(back), part],
            device_id=device(offset), device_id_type=MESH,
        )

    def near_arrival(offset, part):
        blocks = blocks_of(-offset[1], part)
        goal, rows = target_rows[offset[0]]
        where = halo.at[offset[1] + 1, offset[2] + 1, blocks, pl.ds(goal, rows), :]
        return pltpu.make_async_remote_copy(
            src_ref=where, dst_ref=where,
            send_sem=near_send.at[number(offset), part],
            recv_sem=near_recv.at[number(offset), part],
            device_id=device(offset), device_id_type=MESH,
        )

    for load in loads[:2]:
        load.wait()

    def pack(lines_of):
        total = None
        for q, line in enumerate(lines_of):
            spread = lax.dot_general(
                line, place_ref[...], (((0,), (0,)), ((), ())),
                precision=HIGHEST, preferred_element_type=jnp.float32,
            )
            spread = [spread[:, 128 * v : 128 * (v + 1)] for v in range(3)]
            if q:
                spread = [pltpu.roll(s, SLOT * q, 1) for s in spread]
            total = spread if total is None else [t + s for t, s in zip(total, spread)]
        return total

    for block in (1, 2):
        spread = pack([disp_ref[k, block - 1] for k in range(3)])
        for v in range(3):
            packed[v, block] = spread[v]
        halo[1, 1, block, pl.ds(8, cells_x), :] = spread[1]
    pl.semaphore_wait(barrier, expect)
    for offset in offsets:

        @pl.when(inside(offset))
        def _():
            near_copy(offset, 1).start()

    def x_copy(step):
        return pltpu.make_async_remote_copy(
            src_ref=ref_ref.at[pl.ds(sizex - 1 if step > 0 else 0, 1)],
            dst_ref=xhalo.at[pl.ds(0 if step > 0 else 1, 1)],
            send_sem=x_send.at[0 if step > 0 else 1], recv_sem=x_recv.at[0 if step > 0 else 1],
            device_id=device((step, 0, 0)), device_id_type=MESH,
        )

    for load in loads[2:4]:
        load.wait()
    for step in (-1, 1):

        @pl.when(inside((step, 0, 0)))
        def _():
            x_copy(step).start()

    for copy in z_copies:
        copy.start()

    def bin_cell(cell, carry):
        rows = pl.multiple_of(cell * 8, 8)
        total = [None, None]
        for i in range(BIN):
            x = cell * BIN + i
            slabs = (ref_ref[x].astype(jnp.float32), def_ref[x].astype(jnp.float32))
            yrows[0, pl.ds(x, 1), :] = slabs[0][:1]
            yrows[1, pl.ds(x, 1), :] = slabs[0][sizey - 1 :]
            total = [s if t is None else t + s for t, s in zip(total, slabs)]
        for image in range(2):
            for y in range(2):
                binned[2 * image + y, pl.ds(rows, 8), :] = total[image][8 * y : 8 * y + 8]
        return carry

    lax.fori_loop(0, cells_x, bin_cell, 0)
    for load in loads[4:]:
        load.wait()
    spread = None
    for q in range(4):
        line = binned[q, pl.ds(0, cells_x, stride=8), :]
        for s in range(1, 8):
            line = line + binned[q, pl.ds(s, cells_x, stride=8), :]
        part = jnp.dot(line, bin_ref[...], precision=HIGHEST, preferred_element_type=jnp.float32)
        part = [part[:, 128 * v : 128 * (v + 1)] for v in range(3)]
        if q:
            part = [pltpu.roll(p, SLOT * q, 1) for p in part]
        spread = part if spread is None else [a + b for a, b in zip(spread, part)]
    for v in range(3):
        packed[v, 0] = spread[v]
    halo[1, 1, 0, pl.ds(8, cells_x), :] = spread[1]
    for offset in offsets:

        @pl.when(inside(offset))
        def _():
            near_copy(offset, 0).start()

    def y_copy(step):
        side = 1 if step > 0 else 0
        return pltpu.make_async_remote_copy(
            src_ref=ysend.at[side], dst_ref=yhalo.at[1 - side],
            send_sem=y_send.at[side], recv_sem=y_recv.at[1 - side],
            device_id=device((0, step, 0)), device_id_type=MESH,
        )

    ysend[...] = yrows[...].astype(jnp.bfloat16)
    for step in (-1, 1):

        @pl.when(inside((0, step, 0)))
        def _():
            y_copy(step).start()

    for part in (1, 0):
        for offset in offsets:

            @pl.when(inside(offset))
            def _():
                near_arrival(offset, part).wait_recv()

    summed = [[halo[y, 0, b] + halo[y, 1, b] + halo[y, 2, b] for b in range(3)] for y in range(3)]
    rows = cells_x + 16
    lane = lax.broadcasted_iota(jnp.int32, (rows, 128), 1)
    slot = lane // SLOT

    def centred(b, upper):
        one, two = (SLOT, 128 - SLOT) if upper else (128 - SLOT, SLOT)
        ends = jnp.where(slot == 0, pltpu.roll(summed[0][b], one, 1), pltpu.roll(summed[2][b], one, 1))
        return jnp.where(jnp.logical_or(slot == 0, slot == 3), ends, pltpu.roll(summed[1][b], two, 1))

    coarse = centred(0, False)
    deformed = centred(0, True)
    displacement = []
    for k in range(3):
        parts = [
            pltpu.roll(block, SLOT * ((s - k) % 4), 1) if s != k else block
            for s, block in enumerate((summed[0][2], summed[1][1], summed[1][2], summed[2][1]))
        ]
        displacement.append(
            jnp.where(slot < 2, jnp.where(slot == 0, parts[0], parts[1]), jnp.where(slot == 2, parts[2], parts[3]))
        )
    before = jnp.where(slot < 2, summed[0][0], pltpu.roll(summed[1][0], 64, 1))
    after = jnp.where(slot < 2, summed[1][0], pltpu.roll(summed[2][0], 64, 1))
    slopes = [
        (pltpu.roll(coarse, rows - 1, 0) - pltpu.roll(coarse, 1, 0)) * 0.5,
        (after - before) * 0.5,
        (pltpu.roll(coarse, 127, 1) - pltpu.roll(coarse, 1, 1)) * 0.5,
    ]
    mismatch = deformed - coarse - (
        slopes[0] * displacement[0] + slopes[1] * displacement[1] + slopes[2] * displacement[2]
    )
    place = lane - slot * SLOT
    low = jnp.where(me[2] > 0, 1, 2)
    high = jnp.where(me[2] < nz - 1, cells_z + 2, cells_z + 1)
    keep = jnp.logical_and(place >= low, place <= high)
    keep = jnp.logical_and(keep, slot >= jnp.where(me[1] > 0, 0, 1))
    keep = jnp.logical_and(keep, slot <= jnp.where(me[1] < ny - 1, 3, 2))
    rhs = [jnp.where(keep, s * mismatch, 0.0)[8 : 8 + cells_x] for s in slopes]

    mine[...] = jnp.dot(
        sums_ref[...], jnp.concatenate(rhs, axis=0), precision=HIGHEST, preferred_element_type=jnp.float32
    )

    def peer_copy(j):
        return pltpu.make_async_remote_copy(
            src_ref=mine, dst_ref=theirs.at[me[0]],
            send_sem=peer_send.at[j], recv_sem=peer_recv.at[j],
            device_id=peer(j), device_id_type=MESH,
        )

    for j in range(1, nx):
        peer_copy(j).start()

    for step in (-1, 1):

        @pl.when(inside((step, 0, 0)))
        def _():
            x_copy(-step).wait_recv()

        @pl.when(inside((0, step, 0)))
        def _():
            y_copy(-step).wait_recv()

    framed[0] = xhalo[0]
    framed[sizex + 1] = xhalo[1]
    yout[...] = yhalo[...]

    for j in range(1, nx):
        came = pltpu.make_async_remote_copy(
            src_ref=mine, dst_ref=theirs.at[lax.rem(me[0] + nx - j, nx)],
            send_sem=peer_send.at[j], recv_sem=peer_recv.at[j],
            device_id=peer(j), device_id_type=MESH,
        )
        came.wait_recv()

    lane_of = lax.broadcasted_iota(jnp.int32, (cells_z, 128), 1)
    z_of = lax.broadcasted_iota(jnp.int32, (cells_z, 128), 0)
    sums = theirs[...].reshape(8 * nx, 128)
    for k in range(3):
        step = jnp.dot(
            table_ref[k], jnp.concatenate([rhs[k], sums], axis=0),
            precision=HIGHEST, preferred_element_type=jnp.float32,
        )
        new = displacement[k] + step
        for y in range(2):
            new_ref[k, y] = lax.dot_general(
                jnp.where(lane_of == z_of + (SLOT * (y + 1) + 2), 1.0, 0.0), new[8 : 8 + cells_x],
                (((1,), (1,)), ((), ())), precision=HIGHEST, preferred_element_type=jnp.float32,
            )
        along = jnp.dot(new, prolong_ref[...], precision=HIGHEST, preferred_element_type=jnp.float32) * 0.5
        for s in range(4):
            lines[k, s] = along[:, sizez * s : sizez * (s + 1)]

    for copy in z_copies:
        copy.wait_recv()

    for copy in z_copies:
        copy.wait_send()
    for j in range(1, nx):
        peer_copy(j).wait_send()
    for step in (-1, 1):

        @pl.when(inside((step, 0, 0)))
        def _():
            x_copy(step).wait_send()

        @pl.when(inside((0, step, 0)))
        def _():
            y_copy(step).wait_send()

    for offset in offsets:

        @pl.when(inside(offset))
        def _():
            for part in range(2):
                near_copy(offset, part).wait_send()


def combine(
    counts, chunks,
    new_in, lines, refs, defs, yhalo, zhalo,
    new_ref, out_hbm,
    out, out_sem,
):
    nz = counts[2]
    sizex, sizey, sizez = defs.shape
    cells_x = sizex // BIN
    sides = zhalo.shape[0]
    span = sizex // chunks
    at_z = lax.axis_index("gz")
    new_ref[...] = new_in[...]

    row = lax.broadcasted_iota(jnp.int32, (sizez, sizez), 0)
    column = lax.broadcasted_iota(jnp.int32, (sizez, sizez), 1)
    inner = jnp.where(row == column + 1, 1.0, 0.0) - jnp.where(row + 1 == column, 1.0, 0.0)
    from_low = jnp.where(
        jnp.logical_and(jnp.logical_and(row == sizez - 1, column == 0), at_z > 0), -1.0, 0.0
    )
    from_high = jnp.where(
        jnp.logical_and(jnp.logical_and(row == 0, column == sizez - 1), at_z < nz - 1), 1.0, 0.0
    )
    outer = [from_low + from_high] if sides == 1 else [from_low, from_high]
    across = jnp.concatenate([inner] + outer, axis=0).astype(jnp.bfloat16)

    rows = BIN * sizey
    row = lax.broadcasted_iota(jnp.int32, (rows, rows + 16), 0)
    column = lax.broadcasted_iota(jnp.int32, (rows, rows + 16), 1)
    y, slab = row % sizey, row // sizey
    after = jnp.where(y == sizey - 1, rows + 8 + slab, row + 1)
    before = jnp.where(y == 0, rows + slab, row - 1)
    along = (jnp.where(column == after, 1.0, 0.0) - jnp.where(column == before, 1.0, 0.0)).astype(jnp.bfloat16)

    third = lax.broadcasted_iota(jnp.int32, (8, sizez), 0).astype(jnp.float32)
    offset_y = (third + 0.5) / 8.0 - 0.5
    weight_low = jnp.maximum(-offset_y, 0.0)
    weight_high = jnp.maximum(offset_y, 0.0)
    weight_mid = 1.0 - jnp.abs(offset_y)

    def plane(at):
        planes = []
        for k in range(3):
            row_of = [lines[k, s, pl.ds(at, 1), :] for s in range(4)]
            planes.append(
                jnp.concatenate(
                    [
                        weight_low * row_of[c] + weight_mid * row_of[c + 1] + weight_high * row_of[c + 2]
                        for c in range(2)
                    ],
                    axis=0,
                )
            )
        return planes

    def residual(cell, carry):
        past, now = carry
        later = plane(cell + 9)
        start = pl.multiple_of(cell * BIN, BIN)
        own = refs[pl.ds(start + 1, BIN)].reshape(rows, sizez)
        sideways = [own] + [zhalo[i, pl.ds(start, BIN)].reshape(rows, sizez) for i in range(sides)]
        grad_z = jnp.dot(jnp.concatenate(sideways, axis=1), across, preferred_element_type=jnp.float32)
        ends = jnp.concatenate([yhalo[i, pl.ds(start, BIN), :].astype(jnp.float32) for i in range(2)], axis=0)
        grad_y = jnp.dot(
            along, jnp.concatenate([own, ends.astype(jnp.bfloat16)], axis=0), preferred_element_type=jnp.float32
        )
        slabs = [refs[start + i].astype(jnp.float32) for i in range(BIN + 2)]
        for i in range(BIN):
            t = (i + 0.5) / BIN - 0.5
            other = later if t > 0 else past
            field = [n + abs(t) * (o - n) for n, o in zip(now, other)]
            part = slice(i * sizey, (i + 1) * sizey)
            total = defs[start + i].astype(jnp.float32) - slabs[i + 1]
            total = total - (slabs[i + 2] - slabs[i]) * field[0]
            total = total - grad_y[part] * field[1] - grad_z[part] * field[2]
            out[start + i] = total.astype(jnp.bfloat16)
        return (now, later)

    def store(c):
        slabs = pl.ds(c * span, span)
        return pltpu.make_async_copy(out.at[slabs], out_hbm.at[slabs], out_sem.at[c])

    state = (plane(7), plane(8))
    for c in range(chunks):
        each = cells_x // chunks
        state = lax.fori_loop(c * each, (c + 1) * each, residual, state)
        store(c).start()
    for c in range(chunks):
        store(c).wait()


def on_device(counts, ref_image, def_image, displacement):
    nx, ny, nz = counts
    sizex, sizey, sizez = ref_image.shape
    cells_x, cells_z = sizex // BIN, sizez // BIN
    table, sums = inverse_table(nx, cells_x)
    place, binning, prolong = lane_tables(cells_z, sizez, 4)
    sides = 1 if nz == 2 else 2
    dma = pltpu.SemaphoreType.DMA
    vmem, anywhere = pl.BlockSpec(memory_space=pltpu.VMEM), pl.BlockSpec(memory_space=pl.ANY)
    shape = jax.ShapeDtypeStruct
    image = ref_image.shape
    cells = jnp.transpose(displacement, (0, 2, 3, 1))
    constants = (table, sums, place, binning, prolong)
    held = pl.pallas_call(
        functools.partial(exchange, counts),
        out_shape=(
            shape(cells.shape, jnp.float32),
            shape((3, 4, cells_x + 16, sizez), jnp.float32),
            shape((sizex + 2, sizey, sizez), jnp.bfloat16),
            shape(image, jnp.bfloat16),
            shape((2, sizex, sizez), jnp.bfloat16),
            shape((sides,) + image, jnp.bfloat16),
        ),
        in_specs=[pl.BlockSpec(memory_space=pltpu.HBM)] * 8,
        out_specs=(vmem,) * 5 + (anywhere,),
        scratch_shapes=[
            pltpu.VMEM(cells.shape, jnp.float32),
            pltpu.VMEM(table.shape[1:], jnp.float32),
            pltpu.VMEM(sums.shape[1:], jnp.float32),
            pltpu.VMEM(place.shape, jnp.float32),
            pltpu.VMEM(binning.shape, jnp.float32),
            pltpu.VMEM(prolong.shape, jnp.float32),
            pltpu.VMEM((4, cells_x * 8, sizez), jnp.float32),
            pltpu.VMEM((3, 3, cells_x, 128), jnp.float32),
            pltpu.VMEM((3, 3, 3, cells_x + 16, 128), jnp.float32),
            pltpu.VMEM((8, 128), jnp.float32),
            pltpu.VMEM((nx, 8, 128), jnp.float32),
            pltpu.VMEM((2, sizey, sizez), jnp.bfloat16),
            pltpu.VMEM((2, sizex, sizez), jnp.float32),
            pltpu.VMEM((2, sizex, sizez), jnp.bfloat16),
            pltpu.VMEM((2, sizex, sizez), jnp.bfloat16),
            dma((8,)),
            dma((27, 2)), dma((27, 2)), dma((nx,)), dma((nx,)),
            dma((2,)), dma((2,)), dma((2,)), dma((2,)), dma((sides,)), dma((sides,)),
        ],
        compiler_params=pltpu.CompilerParams(
            collective_id=0, has_side_effects=True, vmem_limit_bytes=16 << 20
        ),
    )(*[pltpu.with_memory_space_constraint(jnp.asarray(x), pltpu.HBM) for x in (ref_image, def_image, cells) + constants])
    chunks = 4
    new, residual = pl.pallas_call(
        functools.partial(combine, counts, chunks),
        out_shape=(shape(cells.shape, jnp.float32), shape(image, jnp.bfloat16)),
        in_specs=[vmem] * 6,
        out_specs=(vmem, anywhere),
        scratch_shapes=[pltpu.VMEM(image, jnp.bfloat16), dma((chunks,))],
        compiler_params=pltpu.CompilerParams(vmem_limit_bytes=16 << 20),
    )(*held)
    return jnp.transpose(new, (0, 3, 1, 2)), residual


def solution(mesh):
    counts = tuple(mesh.shape[axis] for axis in ("gx", "gy", "gz"))
    return jax.shard_map(
        functools.partial(on_device, counts),
        mesh=mesh,
        in_specs=(P("gx", "gy", "gz"), P("gx", "gy", "gz"), P(None, "gx", "gy", "gz")),
        out_specs=(P(None, "gx", "gy", "gz"), P("gx", "gy", "gz")),
        check_vma=False,
    )
```

profile of v0, /device:TPU:0, one launch (start us, length us, event | category | flops | bytes accessed | tf_op | source)
XLA Modules:
  0.0 24.1 jit_solution(17697701807987236415)
XLA Ops:
  0.6 16.2 %shard_map.95 = (f32[3,2,16,32]{3,2,1,0:T(8,128)S(1)}, f32[3,4,48,128]{3,2,1,0:T(8,128)S(1)}, bf16[258,16,128]{2,1,0:T(8,128)(2,1)S(1)}, bf16[256,16,128]{2,1,0:...) custom-call(bf16[256,16,128]{2,1,0:T(8,128)(2,1)} %ref_hbm.1, ...), custom_call_target="tpu_custom_call" | custom-call | tf_op jit(solution)/shard_map/pallas_call | solution.py:521
  16.9 7.3 %shard_map.96 = (f32[3,2,16,32]{3,2,1,0:T(8,128)}, bf16[256,16,128]{2,1,0:T(8,128)(2,1)}) custom-call(f32[3,2,16,32]{3,2,1,0:T(8,128)S(1)} %get-tuple-element.10.new_in, f32[3,4,48,128]{3,2,1,0:T(8,128)S(1)} %get-tuple-element.11.lines, bf16[258,16,128]{2,1,0:T(8,128)(2,1)S(1)} %get-tuple-element.12.refs, bf16[256,16,128]{2,1,0:T(8,128)(2,1)S(1)} %get-tuple-element.13.defs, ...), custom_call_target="tpu_custom_call" | custom-call | tf_op jit(solution)/shard_map/pallas_call | solution.py:558
where the time goes:
time: 24.3 us; the launch traced here: 24.1 us
  Pallas kernels  23.5 us (97%)
  between operations  0.64 us (3%)
    pallas_call x1, Pallas kernels, on_device(): pl.pallas_call(functools.partial(exchange, counts), out_shape=(shape(cell...  16.2 us
    pallas_call x1, Pallas kernels, on_device(): pl.pallas_call(functools.partial(combine, counts, chunks), out_shape=(sha...  7.25 us

commit v1 on v0

--- a/solution.py
+++ b/solution.py
@@ -73,15 +73,14 @@
 def exchange(
     counts,
     ref_hbm, def_hbm, disp_hbm, table_hbm, sums_hbm, place_hbm, bin_hbm, prolong_hbm,
-    new_ref, lines, framed, def_ref, yout, zhalo,
-    disp_ref, table_ref, sums_ref, place_ref, bin_ref, prolong_ref,
+    new_ref, lines, base, grad_x, grad_y, grad_z,
+    zhalo, ref_ref, def_ref, disp_ref, table_ref, sums_ref, place_ref, bin_ref, prolong_ref,
     binned, packed, halo, mine, theirs, xhalo, yrows, ysend, yhalo,
     load_sem,
     near_send, near_recv, peer_send, peer_recv, x_send, x_recv, y_send, y_recv, z_send, z_recv,
 ):
     nx, ny, nz = counts
     sizex, sizey, sizez = def_ref.shape
-    ref_ref = framed.at[pl.ds(1, sizex)]
     cells_x, cells_z = sizex // BIN, sizez // BIN
     me = (lax.axis_index("gx"), lax.axis_index("gy"), lax.axis_index("gz"))
 
@@ -289,6 +288,48 @@
         def _():
             y_copy(step).start()
 
+    rows_in = BIN * sizey
+
+    def prepare(cell, carry):
+        start = pl.multiple_of(cell * BIN, BIN)
+        first = jnp.maximum(start - 1, 0)
+        last = jnp.minimum(start + BIN, sizex - 1)
+        slabs = [ref_ref[first].astype(jnp.float32)]
+        slabs += [ref_ref[start + i].astype(jnp.float32) for i in range(BIN)]
+        slabs += [ref_ref[last].astype(jnp.float32)]
+        for i in range(BIN):
+            base[start + i] = def_ref[start + i].astype(jnp.float32) - slabs[i + 1]
+            grad_x[start + i] = slabs[i + 2] - slabs[i]
+        return carry
+
+    lax.fori_loop(0, cells_x, prepare, 0)
+
+    for copy in z_copies:
+        copy.wait_recv()
+
+    at_z = me[2]
+    row = lax.broadcasted_iota(jnp.int32, (sizez, sizez), 0)
+    column = lax.broadcasted_iota(jnp.int32, (sizez, sizez), 1)
+    inner = jnp.where(row == column + 1, 1.0, 0.0) - jnp.where(row + 1 == column, 1.0, 0.0)
+    from_low = jnp.where(
+        jnp.logical_and(jnp.logical_and(row == sizez - 1, column == 0), at_z > 0), -1.0, 0.0
+    )
+    from_high = jnp.where(
+        jnp.logical_and(jnp.logical_and(row == 0, column == sizez - 1), at_z < nz - 1), 1.0, 0.0
+    )
+    outer = [from_low + from_high] if nz == 2 else [from_low, from_high]
+    across = jnp.concatenate([inner] + outer, axis=0).astype(jnp.bfloat16)
+
+    def slope_z(cell, carry):
+        start = pl.multiple_of(cell * BIN, BIN)
+        sideways = [ref_ref[pl.ds(start, BIN)].reshape(rows_in, sizez)]
+        sideways += [zhalo[i, pl.ds(start, BIN)].reshape(rows_in, sizez) for i in range(len(z_steps))]
+        slope = jnp.dot(jnp.concatenate(sideways, axis=1), across, preferred_element_type=jnp.float32)
+        grad_z[pl.ds(start, BIN)] = slope.reshape(BIN, sizey, sizez)
+        return carry
+
+    lax.fori_loop(0, cells_x, slope_z, 0)
+
     for part in (1, 0):
         for offset in offsets:
 
@@ -359,9 +400,22 @@
         def _():
             y_copy(-step).wait_recv()
 
-    framed[0] = xhalo[0]
-    framed[sizex + 1] = xhalo[1]
-    yout[...] = yhalo[...]
+    grad_x[0] = ref_ref[1].astype(jnp.float32) - xhalo[0].astype(jnp.float32)
+    grad_x[sizex - 1] = xhalo[1].astype(jnp.float32) - ref_ref[sizex - 2].astype(jnp.float32)
+    yrows[...] = yhalo[...].astype(jnp.float32)
+    slab_row = lax.broadcasted_iota(jnp.int32, (sizey, sizez), 0)
+
+    def slope_y(cell, carry):
+        start = pl.multiple_of(cell * BIN, BIN)
+        for i in range(BIN):
+            x = start + i
+            slab = ref_ref[x].astype(jnp.float32)
+            above = jnp.where(slab_row == sizey - 1, yrows[1, pl.ds(x, 1), :], pltpu.roll(slab, sizey - 1, 0))
+            below = jnp.where(slab_row == 0, yrows[0, pl.ds(x, 1), :], pltpu.roll(slab, 1, 0))
+            grad_y[x] = above - below
+        return carry
+
+    lax.fori_loop(0, cells_x, slope_y, 0)
 
     for j in range(1, nx):
         came = pltpu.make_async_remote_copy(
@@ -390,9 +444,6 @@
             lines[k, s] = along[:, sizez * s : sizez * (s + 1)]
 
     for copy in z_copies:
-        copy.wait_recv()
-
-    for copy in z_copies:
         copy.wait_send()
     for j in range(1, nx):
         peer_copy(j).wait_send()
@@ -415,38 +466,16 @@
 
 
 def combine(
-    counts, chunks,
-    new_in, lines, refs, defs, yhalo, zhalo,
-    new_ref, out_hbm,
-    out, out_sem,
+    chunks,
+    new_in, lines, base, grad_x, grad_y, grad_z,
+    new_hbm, out_hbm,
+    out, new_sem, out_sem,
 ):
-    nz = counts[2]
-    sizex, sizey, sizez = defs.shape
+    sizex, sizey, sizez = base.shape
     cells_x = sizex // BIN
-    sides = zhalo.shape[0]
     span = sizex // chunks
-    at_z = lax.axis_index("gz")
-    new_ref[...] = new_in[...]
-
-    row = lax.broadcasted_iota(jnp.int32, (sizez, sizez), 0)
-    column = lax.broadcasted_iota(jnp.int32, (sizez, sizez), 1)
-    inner = jnp.where(row == column + 1, 1.0, 0.0) - jnp.where(row + 1 == column, 1.0, 0.0)
-    from_low = jnp.where(
-        jnp.logical_and(jnp.logical_and(row == sizez - 1, column == 0), at_z > 0), -1.0, 0.0
-    )
-    from_high = jnp.where(
-        jnp.logical_and(jnp.logical_and(row == 0, column == sizez - 1), at_z < nz - 1), 1.0, 0.0
-    )
-    outer = [from_low + from_high] if sides == 1 else [from_low, from_high]
-    across = jnp.concatenate([inner] + outer, axis=0).astype(jnp.bfloat16)
-
-    rows = BIN * sizey
-    row = lax.broadcasted_iota(jnp.int32, (rows, rows + 16), 0)
-    column = lax.broadcasted_iota(jnp.int32, (rows, rows + 16), 1)
-    y, slab = row % sizey, row // sizey
-    after = jnp.where(y == sizey - 1, rows + 8 + slab, row + 1)
-    before = jnp.where(y == 0, rows + slab, row - 1)
-    along = (jnp.where(column == after, 1.0, 0.0) - jnp.where(column == before, 1.0, 0.0)).astype(jnp.bfloat16)
+    keep_new = pltpu.make_async_copy(new_in, new_hbm, new_sem.at[0])
+    keep_new.start()
 
     third = lax.broadcasted_iota(jnp.int32, (8, sizez), 0).astype(jnp.float32)
     offset_y = (third + 0.5) / 8.0 - 0.5
@@ -469,40 +498,39 @@
             )
         return planes
 
+    grads = (grad_x, grad_y, grad_z)
+
     def residual(cell, carry):
-        past, now = carry
+        now, rise = carry
         later = plane(cell + 9)
+        climb = [(b - a) * 0.125 for a, b in zip(now, later)]
         start = pl.multiple_of(cell * BIN, BIN)
-        own = refs[pl.ds(start + 1, BIN)].reshape(rows, sizez)
-        sideways = [own] + [zhalo[i, pl.ds(start, BIN)].reshape(rows, sizez) for i in range(sides)]
-        grad_z = jnp.dot(jnp.concatenate(sideways, axis=1), across, preferred_element_type=jnp.float32)
-        ends = jnp.concatenate([yhalo[i, pl.ds(start, BIN), :].astype(jnp.float32) for i in range(2)], axis=0)
-        grad_y = jnp.dot(
-            along, jnp.concatenate([own, ends.astype(jnp.bfloat16)], axis=0), preferred_element_type=jnp.float32
-        )
-        slabs = [refs[start + i].astype(jnp.float32) for i in range(BIN + 2)]
         for i in range(BIN):
-            t = (i + 0.5) / BIN - 0.5
-            other = later if t > 0 else past
-            field = [n + abs(t) * (o - n) for n, o in zip(now, other)]
-            part = slice(i * sizey, (i + 1) * sizey)
-            total = defs[start + i].astype(jnp.float32) - slabs[i + 1]
-            total = total - (slabs[i + 2] - slabs[i]) * field[0]
-            total = total - grad_y[part] * field[1] - grad_z[part] * field[2]
+            if i == 0:
+                field = [n - 3.5 * r for n, r in zip(now, rise)]
+            elif i == BIN // 2:
+                field = [n + 0.5 * c for n, c in zip(now, climb)]
+            else:
+                field = [f + d for f, d in zip(field, rise if i < BIN // 2 else climb)]
+            total = base[start + i]
+            for grad, f in zip(grads, field):
+                total = total - grad[start + i] * f
             out[start + i] = total.astype(jnp.bfloat16)
-        return (now, later)
+        return (later, climb)
 
     def store(c):
         slabs = pl.ds(c * span, span)
         return pltpu.make_async_copy(out.at[slabs], out_hbm.at[slabs], out_sem.at[c])
 
-    state = (plane(7), plane(8))
+    before, now = plane(7), plane(8)
+    state = (now, [(b - a) * 0.125 for a, b in zip(before, now)])
     for c in range(chunks):
         each = cells_x // chunks
         state = lax.fori_loop(c * each, (c + 1) * each, residual, state)
         store(c).start()
     for c in range(chunks):
         store(c).wait()
+    keep_new.wait()
 
 
 def on_device(counts, ref_image, def_image, displacement):
@@ -523,14 +551,17 @@
         out_shape=(
             shape(cells.shape, jnp.float32),
             shape((3, 4, cells_x + 16, sizez), jnp.float32),
-            shape((sizex + 2, sizey, sizez), jnp.bfloat16),
-            shape(image, jnp.bfloat16),
-            shape((2, sizex, sizez), jnp.bfloat16),
-            shape((sides,) + image, jnp.bfloat16),
+            shape(image, jnp.float32),
+            shape(image, jnp.float32),
+            shape(image, jnp.float32),
+            shape(image, jnp.float32),
         ),
         in_specs=[pl.BlockSpec(memory_space=pltpu.HBM)] * 8,
-        out_specs=(vmem,) * 5 + (anywhere,),
+        out_specs=(vmem,) * 6,
         scratch_shapes=[
+            pltpu.VMEM((sides,) + image, jnp.bfloat16),
+            pltpu.VMEM(image, jnp.bfloat16),
+            pltpu.VMEM(image, jnp.bfloat16),
             pltpu.VMEM(cells.shape, jnp.float32),
             pltpu.VMEM(table.shape[1:], jnp.float32),
             pltpu.VMEM(sums.shape[1:], jnp.float32),
@@ -551,16 +582,16 @@
             dma((2,)), dma((2,)), dma((2,)), dma((2,)), dma((sides,)), dma((sides,)),
         ],
         compiler_params=pltpu.CompilerParams(
-            collective_id=0, has_side_effects=True, vmem_limit_bytes=16 << 20
+            collective_id=0, has_side_effects=True, vmem_limit_bytes=24 << 20
         ),
     )(*[pltpu.with_memory_space_constraint(jnp.asarray(x), pltpu.HBM) for x in (ref_image, def_image, cells) + constants])
     chunks = 4
     new, residual = pl.pallas_call(
-        functools.partial(combine, counts, chunks),
+        functools.partial(combine, chunks),
         out_shape=(shape(cells.shape, jnp.float32), shape(image, jnp.bfloat16)),
         in_specs=[vmem] * 6,
-        out_specs=(vmem, anywhere),
-        scratch_shapes=[pltpu.VMEM(image, jnp.bfloat16), dma((chunks,))],
+        out_specs=(anywhere, anywhere),
+        scratch_shapes=[pltpu.VMEM(image, jnp.bfloat16), dma((1,)), dma((chunks,))],
         compiler_params=pltpu.CompilerParams(vmem_limit_bytes=16 << 20),
     )(*held)
     return jnp.transpose(new, (0, 3, 1, 2)), residual

time: 24.3 us -> 20 us (0.82)
  Pallas kernels: 23.5 us -> 19.2 us
    pallas_call x1, Pallas kernels: 7.25 us -> 1.81 us  [on_device(): pl.pallas_call(functools.partial(combine, chunks), out_shape=(shape(cells...]
    pallas_call x1, Pallas kernels: 16.2 us -> 17.4 us  [on_device(): pl.pallas_call(functools.partial(exchange, counts), out_shape=(shape(cell...]
where the time goes in v1:
time: 20 us; the launch traced here: 19.9 us
  Pallas kernels  19.2 us (96%)
  between operations  0.64 us (3%)
    pallas_call x1, Pallas kernels, on_device(): pl.pallas_call(functools.partial(exchange, counts), out_shape=(shape(cell...  17.4 us
    pallas_call x1, Pallas kernels, on_device(): pl.pallas_call(functools.partial(combine, chunks), out_shape=(shape(cells...  1.81 us

profile of v1, /device:TPU:0, one launch (start us, length us, event | category | flops | bytes accessed | tf_op | source)
XLA Modules:
  0.0 19.9 jit_solution(8723298184916289423)
XLA Ops:
  0.6 17.4 %shard_map.95 = (f32[3,2,16,32]{3,2,1,0:T(8,128)S(1)}, f32[3,4,48,128]{3,2,1,0:T(8,128)S(1)}, f32[256,16,128]{2,1,0:T(8,128)S(1)}, f32[256,16,128]{2,1,0:T(8,128...) custom-call(bf16[256,16,128]{2,1,0:T(8,128)(2,1)} %ref_hbm.1, bf16[256,16,128]{2,1,0:T(8,128)(2,1)} %def_hbm.1, ...), custom_call_target="tpu_custom_call" | custom-call | tf_op jit(solution)/shard_map/pallas_call | solution.py:549
  18.0 1.8 %shard_map.96 = (f32[3,2,16,32]{3,2,1,0:T(8,128)}, bf16[256,16,128]{2,1,0:T(8,128)(2,1)}) custom-call(f32[3,2,16,32]{3,2,1,0:T(8,128)S(1)} %get-tuple-element.10.new_in, f32[3,4,48,128]{3,2,1,0:T(8,128)S(1)} %get-tuple-element.11.lines, f32[256,16,128]{2,1,0:T(8,128)S(1)} %get-tuple-element.12.base, f32[256,16,128]{2,1,0:T(8,128)S(1)} %get-tuple-element.13.grad_x, ...), custom_call_target="tpu_custom_call" | custom-call | tf_op jit(solution)/shard_map/pallas_call | solution.py:589

commit v2 on v1

v2 whole, which is shorter than its diff:
```python
import functools

import jax
import jax.numpy as jnp
import numpy as np
from jax import lax
from jax.experimental import pallas as pl
from jax.experimental.pallas import tpu as pltpu
from jax.sharding import PartitionSpec as P

stiffness = 64.0
BIN = 8
SLOT = 32
MESH = pl.DeviceIdType.MESH
half = jnp.bfloat16


def solve_tables(devices, cells, rows):
    lines = devices * cells
    theta = np.arccosh((1.0 + 2.0 * stiffness) / (2.0 * stiffness))
    index = np.arange(lines)
    low = np.minimum(index[:, None], index[None, :])
    high = np.maximum(index[:, None], index[None, :])
    a, b, c = (low + 1) * theta, (lines - high) * theta, (lines + 1) * theta
    inverse = (
        np.exp(a + b - c) * (1 - np.exp(-2 * a)) * (1 - np.exp(-2 * b)) / (1 - np.exp(-2 * c))
        / (2.0 * stiffness * np.sinh(theta))
    )
    solve = np.zeros((devices, 2 * rows, 2 * lines), np.float32)
    pick = np.zeros((devices, rows, 3 * lines), np.float32)
    for me in range(devices):
        first = me * cells
        for row, x in [(r, first + r) for r in range(cells + 1)] + [(rows - 1, first - 1)]:
            if x < 0 or x >= lines:
                continue
            top = inverse[x].astype(half).astype(np.float64)
            solve[me, row, :lines] = top
            solve[me, row, lines:] = top
            solve[me, rows + row, :lines] = inverse[x] - top
            pick[me, row, x::lines] = 1.0
    return solve.astype(half), pick.astype(half)


def lane_tables(cells_z, size_z, deep, slots):
    binning = np.repeat(np.eye(cells_z, dtype=np.float32), BIN, axis=1) / 32.0
    prolong = np.zeros((slots * SLOT, slots * size_z), np.float32)
    for slot in range(slots):
        for fine in range(size_z):
            cell, offset = fine // BIN, (fine % BIN + 0.5) / BIN - 0.5
            other = (cell + (1 if offset >= 0 else -1)) % deep
            prolong[slot * SLOT + cell, slot * size_z + fine] = 0.5 * (1.0 - abs(offset))
            prolong[slot * SLOT + other, slot * size_z + fine] = 0.5 * abs(offset)
    return np.tile(binning, (1, 2)).astype(half), np.tile(prolong, (2, 1)).astype(half)


def pieces(value, count):
    parts = []
    for i in range(count):
        part = value.astype(half)
        parts.append(part)
        if i < count - 1:
            value = value - part.astype(jnp.float32)
    return parts


def across_lanes(a, b):
    return lax.dot_general(a, b, (((1,), (1,)), ((), ())), preferred_element_type=jnp.float32)


def exchange(
    counts, chunks, early,
    ref_hbm, def_hbm, disp_hbm, solve_hbm, pick_hbm, bin_hbm, prolong_hbm,
    new_ref, lines, base, grad_x, grad_y, grad_z,
    zhalo, ref_ref, def_ref, disp_ref, solve_ref, pick_ref, bin_ref, prolong_ref,
    binned, stack, cells, rims, own_rim, moved, moved_rims, own_moved_rim, dline, dsplit, rsplit,
    xhalo, yrows, ysend, yhalo,
    load_sem, image_sem,
    b_send, b_recv, e_send, e_recv, d_send, d_recv, f_send, f_recv,
    x_send, x_recv, y_send, y_recv, z_send, z_recv,
):
    nx, ny, nz = counts
    sizex, sizey, sizez = def_ref.shape
    cells_x, cells_z = sizex // BIN, sizez // BIN
    groups = 128 // cells_x
    across_x = nx * cells_x
    deep = cells.shape[2]
    rows = new_ref.shape[0]
    me = (lax.axis_index("gx"), lax.axis_index("gy"), lax.axis_index("gz"))
    turn = lax.rem(me[0], groups)

    def device(j, dy, dz):
        gz = me[2] + dz if nz > 2 or dz == 0 else 1 - me[2]
        return {"gx": lax.rem(me[0] + j, nx), "gy": me[1] + dy, "gz": gz}

    def guarded(dy, dz, act):
        tests = []
        for at, step, count in ((me[1], dy, ny), (me[2], dz if nz > 2 else 0, nz)):
            if step:
                tests.append(at > 0 if step < 0 else at < count - 1)
        if tests:
            pl.when(functools.reduce(jnp.logical_and, tests))(act)
        else:
            act()

    z_steps = (1,) if nz == 2 else (1, -1)

    def side_out(dz):
        return me[2] if nz == 2 else (0 if dz > 0 else 1)

    def side_in(dz):
        return 1 - me[2] if nz == 2 else (1 if dz > 0 else 0)

    small = [
        pltpu.make_async_copy(hbm, held, load_sem.at[i])
        for i, (hbm, held) in enumerate(
            (
                (disp_hbm, disp_ref), (bin_hbm, bin_ref), (pick_hbm.at[me[0]], pick_ref),
                (solve_hbm.at[me[0]], solve_ref), (prolong_hbm, prolong_ref),
            )
        )
    ]
    span = sizex // chunks
    images = [
        [
            pltpu.make_async_copy(
                hbm.at[pl.ds(c * span, span)], held.at[pl.ds(c * span, span)], image_sem.at[i, c]
            )
            for i, (hbm, held) in enumerate(((ref_hbm, ref_ref), (def_hbm, def_ref)))
        ]
        for c in range(chunks)
    ]
    small[0].start()
    for pair in images:
        for load in pair:
            load.start()
    for load in small[1:]:
        load.start()

    for buffer in (cells, rims, moved, moved_rims, xhalo, yhalo):
        buffer[...] = jnp.zeros_like(buffer)
    if nz > 2:

        @pl.when(me[2] == 0)
        def _():
            zhalo[0] = jnp.zeros(zhalo.shape[1:], half)

        @pl.when(me[2] == nz - 1)
        def _():
            zhalo[1] = jnp.zeros(zhalo.shape[1:], half)

    barrier = pltpu.get_barrier_semaphore()
    for dy in (0, -1, 1):

        def greet(dy=dy):
            for j in range(nx):
                for dz in (0,) + z_steps:
                    if (j, dy, dz) != (0, 0, 0):

                        def hail(j=j, dz=dz):
                            pl.semaphore_signal(barrier, inc=1, device_id=device(j, dy, dz), device_id_type=MESH)

                        guarded(0, dz, hail)

        guarded(dy, 0, greet)

    reach = [
        1 + (at > 0).astype(jnp.int32) + (at < count - 1).astype(jnp.int32)
        for at, count in zip(me, counts)
    ]
    expect = nx * reach[1] * (2 if nz == 2 else reach[2]) - 1

    def remote(src, dst, send, recv, to):
        return pltpu.make_async_remote_copy(
            src_ref=src, dst_ref=dst, send_sem=send, recv_sem=recv, device_id=to, device_id_type=MESH
        )

    small[0].wait()
    for y in range(2):
        tile = jnp.concatenate(
            [disp_ref[k, y] for k in range(3)] + [jnp.zeros((cells_z, 128 - 3 * cells_x), jnp.float32)], axis=1
        )
        tile = pltpu.roll(tile, turn * cells_x, 1)
        moved[1 + y, me[0], pl.ds(0, cells_z)] = tile
        own_moved_rim[0, y] = tile[cells_z - 1 :]
        own_moved_rim[1, y] = tile[:1]

    body = pl.ds(0, cells_z)

    def moved_copy(j, dy):
        here = {0: pl.ds(1, 2), 1: pl.ds(2, 1), -1: pl.ds(1, 1)}[dy]
        there = {0: pl.ds(1, 2), 1: pl.ds(0, 1), -1: pl.ds(3, 1)}[dy]
        return remote(
            moved.at[here, me[0], body], moved.at[there, me[0], body],
            d_send.at[1 + dy], d_recv.at[1 - dy], device(j, dy, 0),
        )

    def moved_rim_copy(j, dy, dz):
        here = {0: pl.ds(0, 2), 1: pl.ds(1, 1), -1: pl.ds(0, 1)}[dy]
        there = {0: pl.ds(1, 2), 1: pl.ds(0, 1), -1: pl.ds(3, 1)}[dy]
        side = side_out(dz)
        return remote(
            own_moved_rim.at[side, here], moved_rims.at[side, there, me[0]],
            f_send.at[side, 1 + dy], f_recv.at[side, 1 - dy], device(j, dy, dz),
        )

    def cell_copy(j, dy):
        return remote(
            cells.at[1, me[0], body], cells.at[1 - dy, me[0], body],
            b_send.at[1 + dy], b_recv.at[1 - dy], device(j, dy, 0),
        )

    def rim_copy(j, dy, dz):
        side = side_out(dz)
        return remote(
            own_rim.at[side], rims.at[side, 1 - dy, me[0]],
            e_send.at[side, 1 + dy], e_recv.at[side, 1 - dy], device(j, dy, dz),
        )

    def start_all(flat, rim):
        for dy in (-1, 1, 0):

            def act(dy=dy):
                for j in list(range(nx - 1, 0, -1)) + ([0] if dy else []):
                    flat(j, dy).start()
                for j in range(nx - 1, -1, -1):
                    for dz in z_steps:
                        guarded(0, dz, lambda j=j, dz=dz: rim(j, dy, dz).start())

            guarded(dy, 0, act)

    def wait_flat(dy, flat_ref, send, recv, sent):
        count = nx if dy else nx - 1
        ref = flat_ref(dy, count)
        copy = remote(ref, ref, send.at[1 + dy], recv.at[1 + dy], device(1, 0, 0))
        copy.wait_send() if sent else copy.wait_recv()

    def wait_rim(dy, dz, rim_ref, send, recv, sent):
        ref = rim_ref(dy)
        copy = remote(
            ref, ref, send.at[side_out(dz), 1 + dy], recv.at[side_in(dz), 1 + dy], device(1, 0, 0)
        )
        copy.wait_send() if sent else copy.wait_recv()

    def wait_all(flat_ref, rim_ref, sems, sent):
        for dy in (0, -1, 1):

            def act(dy=dy):
                wait_flat(dy, flat_ref, sems[0], sems[1], sent)
                for dz in z_steps:
                    guarded(0, dz, lambda dz=dz: wait_rim(dy, dz, rim_ref, sems[2], sems[3], sent))

            guarded(dy, 0, act)

    def cell_ref(dy, count):
        return cells.at[0, pl.ds(0, count), body]

    def rim_ref(dy):
        return rims.at[0, 0]

    def moved_ref(dy, count):
        return moved.at[pl.ds(0, 1 if dy else 2), pl.ds(0, count), body]

    def moved_rim_ref(dy):
        return moved_rims.at[0, pl.ds(0, 1 if dy else 2)]

    def bin_cell(cell, carry):
        at = pl.multiple_of(cell * 8, 8)
        total = [None, None]
        for i in range(BIN):
            x = cell * BIN + i
            slabs = (ref_ref[x].astype(jnp.float32), def_ref[x].astype(jnp.float32))
            yrows[0, pl.ds(x, 1), :] = slabs[0][:1]
            yrows[1, pl.ds(x, 1), :] = slabs[0][sizey - 1 :]
            total = [s if t is None else t + s for t, s in zip(total, slabs)]
        for image in range(2):
            for y in range(2):
                binned[2 * image + y, pl.ds(at, 8), :] = total[image][8 * y : 8 * y + 8]
        return carry

    def bin_chunk(c):
        for load in images[c]:
            load.wait()
        each = cells_x // chunks
        lax.fori_loop(c * each, (c + 1) * each, bin_cell, 0)

    for c in range(early):
        bin_chunk(c)
    pl.semaphore_wait(barrier, expect)
    start_all(moved_copy, moved_rim_copy)
    for c in range(early, chunks):
        bin_chunk(c)

    small[1].wait()
    for q in range(4):
        line = binned[q, pl.ds(0, cells_x, stride=8), :]
        for s in range(1, 8):
            line = line + binned[q, pl.ds(s, cells_x, stride=8), :]
        at = pl.multiple_of(lax.rem(turn + q, groups) * cells_x, cells_x)
        for i, part in enumerate(pieces(line, 2)):
            stack[pl.ds(at, cells_x), pl.ds(i * sizez, sizez)] = part
    tile = across_lanes(bin_ref[...], stack[...])
    cells[1, me[0], body] = tile
    own_rim[0] = tile[cells_z - 2 :]
    own_rim[1] = tile[:2]
    start_all(cell_copy, rim_copy)

    def x_copy(step):
        side = 0 if step > 0 else 1
        return remote(
            ref_ref.at[pl.ds(sizex - 1 if step > 0 else 0, 1)], xhalo.at[pl.ds(side, 1)],
            x_send.at[side], x_recv.at[side],
            {"gx": me[0] + step, "gy": me[1], "gz": me[2]},
        )

    def y_copy(step):
        side = 1 if step > 0 else 0
        return remote(
            ysend.at[side], yhalo.at[1 - side], y_send.at[side], y_recv.at[1 - side], device(0, step, 0)
        )

    def z_copy(dz):
        i = 0 if dz > 0 else 1
        return remote(ref_ref, zhalo.at[i], z_send.at[i], z_recv.at[i], device(0, 0, dz))

    def at_x(step, act):
        pl.when(me[0] > 0 if step < 0 else me[0] < nx - 1)(act)

    ysend[...] = yrows[...].astype(half)
    for step in (-1, 1):
        guarded(step, 0, lambda step=step: y_copy(step).start())
        at_x(step, lambda step=step: x_copy(step).start())
    for dz in z_steps:
        guarded(0, dz, lambda dz=dz: z_copy(dz).start())

    def prepare(cell, carry):
        start = pl.multiple_of(cell * BIN, BIN)
        first = jnp.maximum(start - 1, 0)
        last = jnp.minimum(start + BIN, sizex - 1)
        slabs = [ref_ref[first].astype(jnp.float32)]
        slabs += [ref_ref[start + i].astype(jnp.float32) for i in range(BIN)]
        slabs += [ref_ref[last].astype(jnp.float32)]
        for i in range(BIN):
            base[start + i] = def_ref[start + i].astype(jnp.float32) - slabs[i + 1]
            grad_x[start + i] = slabs[i + 2] - slabs[i]
        return carry

    lax.fori_loop(0, cells_x, prepare, 0)

    group = lax.broadcasted_iota(jnp.int32, (deep, 128), 1) // cells_x

    def gather(tiles, q):
        out = []
        for t in range(nx // groups):
            value = tiles[t * groups + (-q) % groups]
            for g in range(1, groups):
                value = jnp.where(group == g, tiles[t * groups + (g - q) % groups], value)
            out.append(pltpu.roll(value, (groups - q) * cells_x, 1) if q else value)
        return out[0] if len(out) == 1 else jnp.concatenate(out, axis=1)

    blank = jnp.zeros((SLOT - deep, across_x), jnp.float32)

    def split_store(target, k, y, value, count):
        padded = jnp.concatenate([value, blank], axis=0)
        for i, part in enumerate(pieces(padded, count)):
            target[pl.ds((4 * k + y) * SLOT, SLOT), pl.ds(i * across_x, across_x)] = part

    for load in small[2:]:
        load.wait()
    wait_all(moved_ref, moved_rim_ref, (d_send, d_recv, f_send, f_recv), False)
    for y in range(4):
        for i in range(nx):
            moved[y, i, pl.ds(cells_z, 1)] = moved_rims[1, y, i]
            moved[y, i, pl.ds(deep - 1, 1)] = moved_rims[0, y, i]
    for y in range(4):
        tiles = [moved[y, i] for i in range(nx)]
        for k in range(3):
            value = gather(tiles, k)
            dline[k, y] = value
            split_store(dsplit, k, y, value, 3)
    new_ref[...] = across_lanes(pick_ref[...], dsplit[...])

    for dz in z_steps:
        guarded(0, dz, lambda dz=dz: z_copy(-dz if nz > 2 else dz).wait_recv())

    row = lax.broadcasted_iota(jnp.int32, (sizez, sizez), 0)
    column = lax.broadcasted_iota(jnp.int32, (sizez, sizez), 1)
    inner = jnp.where(row == column + 1, 1.0, 0.0) - jnp.where(row + 1 == column, 1.0, 0.0)
    from_low = jnp.where(
        jnp.logical_and(jnp.logical_and(row == sizez - 1, column == 0), me[2] > 0), -1.0, 0.0
    )
    from_high = jnp.where(
        jnp.logical_and(jnp.logical_and(row == 0, column == sizez - 1), me[2] < nz - 1), 1.0, 0.0
    )
    outer = [from_low + from_high] if nz == 2 else [from_low, from_high]
    across = jnp.concatenate([inner] + outer, axis=0).astype(half)

    def slope_z(cell, carry):
        start = pl.multiple_of(cell * BIN, BIN)
        sideways = [ref_ref[pl.ds(start, BIN)].reshape(BIN * sizey, sizez)]
        sideways += [zhalo[i, pl.ds(start, BIN)].reshape(BIN * sizey, sizez) for i in range(len(z_steps))]
        slope = jnp.dot(jnp.concatenate(sideways, axis=1), across, preferred_element_type=jnp.float32)
        grad_z[pl.ds(start, BIN)] = slope.reshape(BIN, sizey, sizez)
        return carry

    lax.fori_loop(0, cells_x, slope_z, 0)

    for step in (-1, 1):
        at_x(step, lambda step=step: x_copy(-step).wait_recv())
        guarded(step, 0, lambda step=step: y_copy(-step).wait_recv())
    grad_x[0] = ref_ref[1].astype(jnp.float32) - xhalo[0].astype(jnp.float32)
    grad_x[sizex - 1] = xhalo[1].astype(jnp.float32) - ref_ref[sizex - 2].astype(jnp.float32)
    yrows[...] = yhalo[...].astype(jnp.float32)
    slab_row = lax.broadcasted_iota(jnp.int32, (sizey, sizez), 0)

    def slope_y(cell, carry):
        start = pl.multiple_of(cell * BIN, BIN)
        for i in range(BIN):
            x = start + i
            slab = ref_ref[x].astype(jnp.float32)
            above = jnp.where(slab_row == sizey - 1, yrows[1, pl.ds(x, 1), :], pltpu.roll(slab, sizey - 1, 0))
            below = jnp.where(slab_row == 0, yrows[0, pl.ds(x, 1), :], pltpu.roll(slab, 1, 0))
            grad_y[x] = above - below
        return carry

    lax.fori_loop(0, cells_x, slope_y, 0)

    wait_all(cell_ref, rim_ref, (b_send, b_recv, e_send, e_recv), False)
    for dy in range(3):
        for i in range(nx):
            cells[dy, i, pl.ds(cells_z, 2)] = rims[1, dy, i]
            cells[dy, i, pl.ds(deep - 2, 2)] = rims[0, dy, i]
    tiles = [[cells[dy, i] for i in range(nx)] for dy in range(3)]
    coarse = [gather(tiles[dy], q) for dy in range(3) for q in range(2)]
    deformed = [gather(tiles[dy], q) for dy, q in ((0, 3), (1, 2), (1, 3), (2, 2))]
    lane = lax.broadcasted_iota(jnp.int32, (deep, across_x), 1)
    for y in range(4):
        c = coarse[y + 1]
        slopes = [
            (
                jnp.where(lane == across_x - 1, 0.0, pltpu.roll(c, across_x - 1, 1))
                - jnp.where(lane == 0, 0.0, pltpu.roll(c, 1, 1))
            ) * 0.5,
            (coarse[y + 2] - coarse[y]) * 0.5,
            (pltpu.roll(c, deep - 1, 0) - pltpu.roll(c, 1, 0)) * 0.5,
        ]
        mismatch = deformed[y] - c - (
            slopes[0] * dline[0, y] + slopes[1] * dline[1, y] + slopes[2] * dline[2, y]
        )
        for k in range(3):
            split_store(rsplit, k, y, slopes[k] * mismatch, 2)
    step = across_lanes(solve_ref[...], rsplit[...])
    new = new_ref[...] + (step[:rows] + step[rows:])
    new_ref[...] = new
    parts = [
        jnp.concatenate(pieces(new[:, 4 * SLOT * k : 4 * SLOT * (k + 1)], 2), axis=1) for k in range(3)
    ]
    along = jnp.dot(jnp.concatenate(parts, axis=0), prolong_ref[...], preferred_element_type=jnp.float32)
    for k in range(3):
        for s in range(4):
            lines[k, s] = along[rows * k : rows * (k + 1), sizez * s : sizez * (s + 1)]

    wait_all(moved_ref, moved_rim_ref, (d_send, d_recv, f_send, f_recv), True)
    wait_all(cell_ref, rim_ref, (b_send, b_recv, e_send, e_recv), True)
    for step in (-1, 1):
        guarded(step, 0, lambda step=step: y_copy(step).wait_send())
        at_x(step, lambda step=step: x_copy(step).wait_send())
    for dz in z_steps:
        guarded(0, dz, lambda dz=dz: z_copy(dz).wait_send())


def combine(
    chunks,
    new_in, lines, base, grad_x, grad_y, grad_z,
    new_hbm, out_hbm,
    out, turned, new_sem, out_sem,
):
    sizex, sizey, sizez = base.shape
    cells_x = sizex // BIN
    span = sizex // chunks
    keep_new = pltpu.make_async_copy(turned, new_hbm, new_sem.at[0])
    cells_z = sizez // BIN
    before_row = new_in.shape[0] - 1

    third = lax.broadcasted_iota(jnp.int32, (8, sizez), 0).astype(jnp.float32)
    offset_y = (third + 0.5) / 8.0 - 0.5
    weight_low = jnp.maximum(-offset_y, 0.0)
    weight_high = jnp.maximum(offset_y, 0.0)
    weight_mid = 1.0 - jnp.abs(offset_y)

    def plane(at):
        planes = []
        for k in range(3):
            row_of = [lines[k, s, pl.ds(at, 1), :] for s in range(4)]
            planes.append(
                jnp.concatenate(
                    [
                        weight_low * row_of[c] + weight_mid * row_of[c + 1] + weight_high * row_of[c + 2]
                        for c in range(2)
                    ],
                    axis=0,
                )
            )
        return planes

    grads = (grad_x, grad_y, grad_z)

    def residual(cell, carry):
        now, rise = carry
        later = plane(cell + 1)
        climb = [(b - a) * 0.125 for a, b in zip(now, later)]
        start = pl.multiple_of(cell * BIN, BIN)
        for i in range(BIN):
            if i == 0:
                field = [n - 3.5 * r for n, r in zip(now, rise)]
            elif i == BIN // 2:
                field = [n + 0.5 * c for n, c in zip(now, climb)]
            else:
                field = [f + d for f, d in zip(field, rise if i < BIN // 2 else climb)]
            total = base[start + i]
            for grad, f in zip(grads, field):
                total = total - grad[start + i] * f
            out[start + i] = total.astype(jnp.bfloat16)
        return (later, climb)

    def store(c):
        slabs = pl.ds(c * span, span)
        return pltpu.make_async_copy(out.at[slabs], out_hbm.at[slabs], out_sem.at[c])

    before, now = plane(before_row), plane(0)
    state = (now, [(b - a) * 0.125 for a, b in zip(before, now)])
    for c in range(chunks):
        each = cells_x // chunks
        state = lax.fori_loop(c * each, (c + 1) * each, residual, state)
        store(c).start()
        if c == 0:
            for k in range(3):
                flipped = new_in[:cells_x, 4 * SLOT * k : 4 * SLOT * (k + 1)].T
                for y in range(2):
                    turned[k, y] = flipped[SLOT * (y + 1) : SLOT * (y + 1) + cells_z]
            keep_new.start()
    for c in range(chunks):
        store(c).wait()
    keep_new.wait()


def on_device(counts, ref_image, def_image, displacement):
    nx, ny, nz = counts
    sizex, sizey, sizez = ref_image.shape
    cells_x, cells_z = sizex // BIN, sizez // BIN
    rows, deep, across_x = cells_x + 16, cells_z + 8, nx * cells_x
    solve, pick = solve_tables(nx, cells_x, rows)
    binning, prolong = lane_tables(cells_z, sizez, deep, 4)
    sides = 1 if nz == 2 else 2
    dma = pltpu.SemaphoreType.DMA
    vmem, anywhere = pl.BlockSpec(memory_space=pltpu.VMEM), pl.BlockSpec(memory_space=pl.ANY)
    shape = jax.ShapeDtypeStruct
    image = ref_image.shape
    coarse = jnp.transpose(displacement, (0, 2, 3, 1))
    constants = (solve, pick, binning, prolong)
    f32 = jnp.float32
    held = pl.pallas_call(
        functools.partial(exchange, counts, 4, 2),
        out_shape=(
            shape((rows, 12 * SLOT), f32),
            shape((3, 4, rows, sizez), f32),
            shape(image, f32),
            shape(image, f32),
            shape(image, f32),
            shape(image, f32),
        ),
        in_specs=[pl.BlockSpec(memory_space=pltpu.HBM)] * 7,
        out_specs=(vmem,) * 6,
        scratch_shapes=[
            pltpu.VMEM((sides,) + image, half),
            pltpu.VMEM(image, half),
            pltpu.VMEM(image, half),
            pltpu.VMEM(coarse.shape, f32),
            pltpu.VMEM(solve.shape[1:], half),
            pltpu.VMEM(pick.shape[1:], half),
            pltpu.VMEM(binning.shape, half),
            pltpu.VMEM(prolong.shape, half),
            pltpu.VMEM((4, cells_x * 8, sizez), f32),
            pltpu.VMEM((4 * cells_x, 2 * sizez), half),
            pltpu.VMEM((3, nx, deep, 128), f32),
            pltpu.VMEM((2, 3, nx, 2, 128), f32),
            pltpu.VMEM((2, 2, 128), f32),
            pltpu.VMEM((4, nx, deep, 128), f32),
            pltpu.VMEM((2, 4, nx, 1, 128), f32),
            pltpu.VMEM((2, 2, 1, 128), f32),
            pltpu.VMEM((3, 4, deep, across_x), f32),
            pltpu.VMEM((12 * SLOT, 3 * across_x), half),
            pltpu.VMEM((12 * SLOT, 2 * across_x), half),
            pltpu.VMEM((2, sizey, sizez), half),
            pltpu.VMEM((2, sizex, sizez), f32),
            pltpu.VMEM((2, sizex, sizez), half),
            pltpu.VMEM((2, sizex, sizez), half),
            dma((5,)), dma((2, 4)),
            dma((3,)), dma((3,)), dma((2, 3)), dma((2, 3)),
            dma((3,)), dma((3,)), dma((2, 3)), dma((2, 3)),
            dma((2,)), dma((2,)), dma((2,)), dma((2,)), dma((sides,)), dma((sides,)),
        ],
        compiler_params=pltpu.CompilerParams(
            collective_id=0, has_side_effects=True, vmem_limit_bytes=24 << 20
        ),
    )(*[pltpu.with_memory_space_constraint(jnp.asarray(x), pltpu.HBM) for x in (ref_image, def_image, coarse) + constants])
    chunks = 4
    new, residual = pl.pallas_call(
        functools.partial(combine, chunks),
        out_shape=(shape(coarse.shape, f32), shape(image, half)),
        in_specs=[vmem] * 6,
        out_specs=(anywhere, anywhere),
        scratch_shapes=[pltpu.VMEM(image, half), pltpu.VMEM(coarse.shape, f32), dma((1,)), dma((chunks,))],
        compiler_params=pltpu.CompilerParams(vmem_limit_bytes=16 << 20),
    )(*held)
    return jnp.transpose(new, (0, 3, 1, 2)), residual


def solution(mesh):
    counts = tuple(mesh.shape[axis] for axis in ("gx", "gy", "gz"))
    return jax.shard_map(
        functools.partial(on_device, counts),
        mesh=mesh,
        in_specs=(P("gx", "gy", "gz"), P("gx", "gy", "gz"), P(None, "gx", "gy", "gz")),
        out_specs=(P(None, "gx", "gy", "gz"), P("gx", "gy", "gz")),
        check_vma=False,
    )
```

time: 20 us -> 18.6 us (0.930)
  Pallas kernels: 19.2 us -> 17.8 us
    pallas_call x2, Pallas kernels: 19.2 us -> 17.8 us  [the longest x1 15.8 us: on_device(): pl.pallas_call(functools.partial(exchange, counts, 4, 2), out_shape=(shap...]
where the time goes in v2:
time: 18.6 us; the launch traced here: 18.4 us
  Pallas kernels  17.8 us (96%)
  between operations  0.64 us (3%)
    pallas_call x1, Pallas kernels, on_device(): pl.pallas_call(functools.partial(exchange, counts, 4, 2), out_shape=(shap...  15.8 us
    pallas_call x1, Pallas kernels, on_device(): pl.pallas_call(functools.partial(combine, chunks), out_shape=(shape(coars...  1.92 us

profile of v2, /device:TPU:0, one launch (start us, length us, event | category | flops | bytes accessed | tf_op | source)
XLA Modules:
  0.0 18.4 jit_solution(12035187410236615981)
XLA Ops:
  0.6 15.8 %shard_map.86 = (f32[48,384]{1,0:T(8,128)S(1)}, f32[3,4,48,128]{3,2,1,0:T(8,128)S(1)}, f32[256,16,128]{2,1,0:T(8,128)S(1)}, f32[256,16,128]{2,1,0:T(8,128)S(1)},...) custom-call(bf16[256,16,128]{2,1,0:T(8,128)(2,1)} %ref_hbm.1, bf16[256,16,128]{2,1,0:T(8,128)(2,1)} %def_hbm.1, ...), custom_call_target="tpu_custom_call" | custom-call | tf_op jit(solution)/shard_map/pallas_call | solution.py:561
  16.5 1.9 %shard_map.87 = (f32[3,2,16,32]{3,2,1,0:T(8,128)}, bf16[256,16,128]{2,1,0:T(8,128)(2,1)}) custom-call(f32[48,384]{1,0:T(8,128)S(1)} %get-tuple-element.10.new_in, f32[3,4,48,128]{3,2,1,0:T(8,128)S(1)} %get-tuple-element.11.lines, f32[256,16,128]{2,1,0:T(8,128)S(1)} %get-tuple-element.12.base, f32[256,16,128]{2,1,0:T(8,128)S(1)} %get-tuple-element.13.grad_x, ...), custom_call_target="tpu_custom_call" | custom-call | tf_op jit(solution)/shard_map/pallas_call | solution.py:607

commit v3 on v2

--- a/solution.py
+++ b/solution.py
@@ -50,7 +50,7 @@
             other = (cell + (1 if offset >= 0 else -1)) % deep
             prolong[slot * SLOT + cell, slot * size_z + fine] = 0.5 * (1.0 - abs(offset))
             prolong[slot * SLOT + other, slot * size_z + fine] = 0.5 * abs(offset)
-    return np.tile(binning, (1, 2)).astype(half), np.tile(prolong, (2, 1)).astype(half)
+    return np.tile(binning, (1, 3)).astype(half), np.tile(prolong, (2, 1)).astype(half)
 
 
 def pieces(value, count):
@@ -110,6 +110,21 @@
     def side_in(dz):
         return 1 - me[2] if nz == 2 else (1 if dz > 0 else 0)
 
+    barrier = pltpu.get_barrier_semaphore()
+    for dy in (0, -1, 1):
+
+        def greet(dy=dy):
+            for j in range(nx):
+                for dz in (0,) + z_steps:
+                    if (j, dy, dz) != (0, 0, 0):
+
+                        def hail(j=j, dz=dz):
+                            pl.semaphore_signal(barrier, inc=1, device_id=device(j, dy, dz), device_id_type=MESH)
+
+                        guarded(0, dz, hail)
+
+        guarded(dy, 0, greet)
+
     small = [
         pltpu.make_async_copy(hbm, held, load_sem.at[i])
         for i, (hbm, held) in enumerate(
@@ -136,32 +151,27 @@
     for load in small[1:]:
         load.start()
 
-    for buffer in (cells, rims, moved, moved_rims, xhalo, yhalo):
-        buffer[...] = jnp.zeros_like(buffer)
+    def clear(test, *parts):
+        @pl.when(test)
+        def _():
+            for part in parts:
+                part[...] = jnp.zeros(part.shape, part.dtype)
+
+    low_y, high_y = me[1] == 0, me[1] == ny - 1
+    low_z, high_z = me[2] == 0, me[2] == nz - 1
+    clear(me[0] == 0, xhalo.at[0])
+    clear(me[0] == nx - 1, xhalo.at[1])
+    clear(low_y, yhalo.at[0], cells.at[0], moved.at[0], rims.at[:, 0], moved_rims.at[:, 0])
+    clear(high_y, yhalo.at[1], cells.at[2], moved.at[3], rims.at[:, 2], moved_rims.at[:, 3])
+    clear(low_z, rims.at[0], moved_rims.at[0])
+    clear(high_z, rims.at[1], moved_rims.at[1])
     if nz > 2:
-
-        @pl.when(me[2] == 0)
-        def _():
-            zhalo[0] = jnp.zeros(zhalo.shape[1:], half)
-
-        @pl.when(me[2] == nz - 1)
-        def _():
-            zhalo[1] = jnp.zeros(zhalo.shape[1:], half)
-
-    barrier = pltpu.get_barrier_semaphore()
-    for dy in (0, -1, 1):
-
-        def greet(dy=dy):
-            for j in range(nx):
-                for dz in (0,) + z_steps:
-                    if (j, dy, dz) != (0, 0, 0):
-
-                        def hail(j=j, dz=dz):
-                            pl.semaphore_signal(barrier, inc=1, device_id=device(j, dy, dz), device_id_type=MESH)
-
-                        guarded(0, dz, hail)
-
-        guarded(dy, 0, greet)
+        clear(low_z, zhalo.at[0])
+        clear(high_z, zhalo.at[1])
+    for tiles in (cells, moved):
+        for line in range(tiles.shape[0]):
+            for i in range(nx):
+                tiles[line, i, pl.ds(cells_z, deep - cells_z)] = jnp.zeros((deep - cells_z, 128), jnp.float32)
 
     reach = [
         1 + (at > 0).astype(jnp.int32) + (at < count - 1).astype(jnp.int32)
@@ -285,8 +295,6 @@
 
     for c in range(early):
         bin_chunk(c)
-    pl.semaphore_wait(barrier, expect)
-    start_all(moved_copy, moved_rim_copy)
     for c in range(early, chunks):
         bin_chunk(c)
 
@@ -296,12 +304,14 @@
         for s in range(1, 8):
             line = line + binned[q, pl.ds(s, cells_x, stride=8), :]
         at = pl.multiple_of(lax.rem(turn + q, groups) * cells_x, cells_x)
-        for i, part in enumerate(pieces(line, 2)):
+        for i, part in enumerate(pieces(line, 3)):
             stack[pl.ds(at, cells_x), pl.ds(i * sizez, sizez)] = part
     tile = across_lanes(bin_ref[...], stack[...])
     cells[1, me[0], body] = tile
     own_rim[0] = tile[cells_z - 2 :]
     own_rim[1] = tile[:2]
+    pl.semaphore_wait(barrier, expect)
+    start_all(moved_copy, moved_rim_copy)
     start_all(cell_copy, rim_copy)
 
     def x_copy(step):
@@ -345,6 +355,51 @@
         return carry
 
     lax.fori_loop(0, cells_x, prepare, 0)
+
+    for dz in z_steps:
+        guarded(0, dz, lambda dz=dz: z_copy(-dz if nz > 2 else dz).wait_recv())
+
+    row = lax.broadcasted_iota(jnp.int32, (sizez, sizez), 0)
+    column = lax.broadcasted_iota(jnp.int32, (sizez, sizez), 1)
+    inner = jnp.where(row == column + 1, 1.0, 0.0) - jnp.where(row + 1 == column, 1.0, 0.0)
+    from_low = jnp.where(
+        jnp.logical_and(jnp.logical_and(row == sizez - 1, column == 0), me[2] > 0), -1.0, 0.0
+    )
+    from_high = jnp.where(
+        jnp.logical_and(jnp.logical_and(row == 0, column == sizez - 1), me[2] < nz - 1), 1.0, 0.0
+    )
+    outer = [from_low + from_high] if nz == 2 else [from_low, from_high]
+    across = jnp.concatenate([inner] + outer, axis=0).astype(half)
+
+    def slope_z(cell, carry):
+        start = pl.multiple_of(cell * BIN, BIN)
+        sideways = [ref_ref[pl.ds(start, BIN)].reshape(BIN * sizey, sizez)]
+        sideways += [zhalo[i, pl.ds(start, BIN)].reshape(BIN * sizey, sizez) for i in range(len(z_steps))]
+        slope = jnp.dot(jnp.concatenate(sideways, axis=1), across, preferred_element_type=jnp.float32)
+        grad_z[pl.ds(start, BIN)] = slope.reshape(BIN, sizey, sizez)
+        return carry
+
+    lax.fori_loop(0, cells_x, slope_z, 0, unroll=8)
+
+    for step in (-1, 1):
+        at_x(step, lambda step=step: x_copy(-step).wait_recv())
+        guarded(step, 0, lambda step=step: y_copy(-step).wait_recv())
+    grad_x[0] = ref_ref[1].astype(jnp.float32) - xhalo[0].astype(jnp.float32)
+    grad_x[sizex - 1] = xhalo[1].astype(jnp.float32) - ref_ref[sizex - 2].astype(jnp.float32)
+    yrows[...] = yhalo[...].astype(jnp.float32)
+    slab_row = lax.broadcasted_iota(jnp.int32, (sizey, sizez), 0)
+
+    def slope_y(cell, carry):
+        start = pl.multiple_of(cell * BIN, BIN)
+        for i in range(BIN):
+            x = start + i
+            slab = ref_ref[x].astype(jnp.float32)
+            above = jnp.where(slab_row == sizey - 1, yrows[1, pl.ds(x, 1), :], pltpu.roll(slab, sizey - 1, 0))
+            below = jnp.where(slab_row == 0, yrows[0, pl.ds(x, 1), :], pltpu.roll(slab, 1, 0))
+            grad_y[x] = above - below
+        return carry
+
+    lax.fori_loop(0, cells_x, slope_y, 0)
 
     group = lax.broadcasted_iota(jnp.int32, (deep, 128), 1) // cells_x
 
@@ -378,51 +433,6 @@
             dline[k, y] = value
             split_store(dsplit, k, y, value, 3)
     new_ref[...] = across_lanes(pick_ref[...], dsplit[...])
-
-    for dz in z_steps:
-        guarded(0, dz, lambda dz=dz: z_copy(-dz if nz > 2 else dz).wait_recv())
-
-    row = lax.broadcasted_iota(jnp.int32, (sizez, sizez), 0)
-    column = lax.broadcasted_iota(jnp.int32, (sizez, sizez), 1)
-    inner = jnp.where(row == column + 1, 1.0, 0.0) - jnp.where(row + 1 == column, 1.0, 0.0)
-    from_low = jnp.where(
-        jnp.logical_and(jnp.logical_and(row == sizez - 1, column == 0), me[2] > 0), -1.0, 0.0
-    )
-    from_high = jnp.where(
-        jnp.logical_and(jnp.logical_and(row == 0, column == sizez - 1), me[2] < nz - 1), 1.0, 0.0
-    )
-    outer = [from_low + from_high] if nz == 2 else [from_low, from_high]
-    across = jnp.concatenate([inner] + outer, axis=0).astype(half)
-
-    def slope_z(cell, carry):
-        start = pl.multiple_of(cell * BIN, BIN)
-        sideways = [ref_ref[pl.ds(start, BIN)].reshape(BIN * sizey, sizez)]
-        sideways += [zhalo[i, pl.ds(start, BIN)].reshape(BIN * sizey, sizez) for i in range(len(z_steps))]
-        slope = jnp.dot(jnp.concatenate(sideways, axis=1), across, preferred_element_type=jnp.float32)
-        grad_z[pl.ds(start, BIN)] = slope.reshape(BIN, sizey, sizez)
-        return carry
-
-    lax.fori_loop(0, cells_x, slope_z, 0)
-
-    for step in (-1, 1):
-        at_x(step, lambda step=step: x_copy(-step).wait_recv())
-        guarded(step, 0, lambda step=step: y_copy(-step).wait_recv())
-    grad_x[0] = ref_ref[1].astype(jnp.float32) - xhalo[0].astype(jnp.float32)
-    grad_x[sizex - 1] = xhalo[1].astype(jnp.float32) - ref_ref[sizex - 2].astype(jnp.float32)
-    yrows[...] = yhalo[...].astype(jnp.float32)
-    slab_row = lax.broadcasted_iota(jnp.int32, (sizey, sizez), 0)
-
-    def slope_y(cell, carry):
-        start = pl.multiple_of(cell * BIN, BIN)
-        for i in range(BIN):
-            x = start + i
-            slab = ref_ref[x].astype(jnp.float32)
-            above = jnp.where(slab_row == sizey - 1, yrows[1, pl.ds(x, 1), :], pltpu.roll(slab, sizey - 1, 0))
-            below = jnp.where(slab_row == 0, yrows[0, pl.ds(x, 1), :], pltpu.roll(slab, 1, 0))
-            grad_y[x] = above - below
-        return carry
-
-    lax.fori_loop(0, cells_x, slope_y, 0)
 
     wait_all(cell_ref, rim_ref, (b_send, b_recv, e_send, e_recv), False)
     for dy in range(3):
@@ -559,7 +569,7 @@
     constants = (solve, pick, binning, prolong)
     f32 = jnp.float32
     held = pl.pallas_call(
-        functools.partial(exchange, counts, 4, 2),
+        functools.partial(exchange, counts, 4, 4),
         out_shape=(
             shape((rows, 12 * SLOT), f32),
             shape((3, 4, rows, sizez), f32),
@@ -580,7 +590,7 @@
             pltpu.VMEM(binning.shape, half),
             pltpu.VMEM(prolong.shape, half),
             pltpu.VMEM((4, cells_x * 8, sizez), f32),
-            pltpu.VMEM((4 * cells_x, 2 * sizez), half),
+            pltpu.VMEM((4 * cells_x, 3 * sizez), half),
             pltpu.VMEM((3, nx, deep, 128), f32),
             pltpu.VMEM((2, 3, nx, 2, 128), f32),
             pltpu.VMEM((2, 2, 128), f32),

time: 18.6 us -> 15.2 us (0.82)
  Pallas kernels: 17.8 us -> 14.4 us
    pallas_call x1, Pallas kernels: 15.8 us -> 12.5 us  [on_device(): pl.pallas_call(functools.partial(exchange, counts, 4, 4), out_shape=(shap...]
where the time goes in v3:
time: 15.2 us; the launch traced here: 15.1 us
  Pallas kernels  14.4 us (95%)
  between operations  0.64 us (4%)
    pallas_call x1, Pallas kernels, on_device(): pl.pallas_call(functools.partial(exchange, counts, 4, 4), out_shape=(shap...  12.5 us
    pallas_call x1, Pallas kernels, on_device(): pl.pallas_call(functools.partial(combine, chunks), out_shape=(shape(coars...  1.92 us

profile of v3, /device:TPU:0, one launch (start us, length us, event | category | flops | bytes accessed | tf_op | source)
XLA Modules:
  0.0 15.1 jit_solution(13351700974313068667)
XLA Ops:
  0.6 12.5 %shard_map.86 = (f32[48,384]{1,0:T(8,128)S(1)}, f32[3,4,48,128]{3,2,1,0:T(8,128)S(1)}, f32[256,16,128]{2,1,0:T(8,128)S(1)}, f32[256,16,128]{2,1,0:T(8,128)S(1)},...) custom-call(bf16[256,16,128]{2,1,0:T(8,128)(2,1)} %ref_hbm.1, bf16[256,16,128]{2,1,0:T(8,128)(2,1)} %def_hbm.1, ...), custom_call_target="tpu_custom_call" | custom-call | tf_op jit(solution)/shard_map/pallas_call | solution.py:571
  13.2 1.9 %shard_map.87 = (f32[3,2,16,32]{3,2,1,0:T(8,128)}, bf16[256,16,128]{2,1,0:T(8,128)(2,1)}) custom-call(f32[48,384]{1,0:T(8,128)S(1)} %get-tuple-element.10.new_in, f32[3,4,48,128]{3,2,1,0:T(8,128)S(1)} %get-tuple-element.11.lines, f32[256,16,128]{2,1,0:T(8,128)S(1)} %get-tuple-element.12.base, f32[256,16,128]{2,1,0:T(8,128)S(1)} %get-tuple-element.13.grad_x, ...), custom_call_target="tpu_custom_call" | custom-call | tf_op jit(solution)/shard_map/pallas_call | solution.py:617

commit v4 on v3

v4 whole, which is shorter than its diff:
```python
import functools

import jax
import jax.numpy as jnp
import numpy as np
from jax import lax
from jax.experimental import pallas as pl
from jax.experimental.pallas import tpu as pltpu
from jax.sharding import PartitionSpec as P

stiffness = 64.0
BIN = 8
SLOT = 32
MESH = pl.DeviceIdType.MESH
half = jnp.bfloat16


def solve_tables(devices, cells, rows):
    lines = devices * cells
    theta = np.arccosh((1.0 + 2.0 * stiffness) / (2.0 * stiffness))
    index = np.arange(lines)
    low = np.minimum(index[:, None], index[None, :])
    high = np.maximum(index[:, None], index[None, :])
    a, b, c = (low + 1) * theta, (lines - high) * theta, (lines + 1) * theta
    inverse = (
        np.exp(a + b - c) * (1 - np.exp(-2 * a)) * (1 - np.exp(-2 * b)) / (1 - np.exp(-2 * c))
        / (2.0 * stiffness * np.sinh(theta))
    )
    solve = np.zeros((devices, 2 * rows, 2 * lines), np.float32)
    pick = np.zeros((devices, rows, 3 * lines), np.float32)
    for me in range(devices):
        first = me * cells
        for row, x in [(r, first + r) for r in range(cells + 1)] + [(rows - 1, first - 1)]:
            if x < 0 or x >= lines:
                continue
            top = inverse[x].astype(half).astype(np.float64)
            solve[me, row, :lines] = top
            solve[me, row, lines:] = top
            solve[me, rows + row, :lines] = inverse[x] - top
            pick[me, row, x::lines] = 1.0
    return solve.astype(half), pick.astype(half)


def lane_tables(cells_z, size_z, deep, slots):
    binning = np.repeat(np.eye(cells_z, dtype=np.float32), BIN, axis=1) / 32.0
    prolong = np.zeros((slots * SLOT, slots * size_z), np.float32)
    for slot in range(slots):
        for fine in range(size_z):
            cell, offset = fine // BIN, (fine % BIN + 0.5) / BIN - 0.5
            other = (cell + (1 if offset >= 0 else -1)) % deep
            prolong[slot * SLOT + cell, slot * size_z + fine] = 0.5 * (1.0 - abs(offset))
            prolong[slot * SLOT + other, slot * size_z + fine] = 0.5 * abs(offset)
    return np.tile(binning, (1, 3)).astype(half), np.tile(prolong, (2, 1)).astype(half)


def pieces(value, count):
    parts = []
    for i in range(count):
        part = value.astype(half)
        parts.append(part)
        if i < count - 1:
            value = value - part.astype(jnp.float32)
    return parts


def across_lanes(a, b):
    return lax.dot_general(a, b, (((1,), (1,)), ((), ())), preferred_element_type=jnp.float32)


def exchange(
    counts, chunks, parts_of,
    ref_hbm, def_hbm, disp_hbm, table_hbm,
    new_ref, lines, base, grad_x, grad_y, grad_z,
    zhalo, image_ref, disp_ref, table_ref,
    binned, stack, mail, rims, own_rim, foot, dline, cline, fline, dsplit, rsplit,
    xhalo, yrows, ysend, yhalo,
    load_sem, image_sem, mail_send, mail_recv, y_recv, z_recv,
):
    nx, ny, nz = counts
    ref_ref, def_ref = image_ref.at[0], image_ref.at[1]
    sizex, sizey, sizez = def_ref.shape
    cells_x, cells_z = sizex // BIN, sizez // BIN
    groups = 128 // cells_x
    across_x = nx * cells_x
    deep = dline.shape[2]
    rows = new_ref.shape[0]
    me = (lax.axis_index("gx"), lax.axis_index("gy"), lax.axis_index("gz"))
    turn = lax.rem(me[0], groups)

    def device(j, dy, dz):
        gz = me[2] + dz if nz > 2 or dz == 0 else 1 - me[2]
        return {"gx": lax.rem(me[0] + j, nx), "gy": me[1] + dy, "gz": gz}

    def guarded(dy, dz, act):
        tests = []
        for at, step, count in ((me[1], dy, ny), (me[2], dz if nz > 2 else 0, nz)):
            if step:
                tests.append(at > 0 if step < 0 else at < count - 1)
        if tests:
            pl.when(functools.reduce(jnp.logical_and, tests))(act)
        else:
            act()

    z_steps = (1,) if nz == 2 else (1, -1)

    def side_out(dz):
        return me[2] if nz == 2 else (0 if dz > 0 else 1)

    def lane_of(dz):
        return 0 if nz == 2 or dz == 0 else (1 if dz > 0 else 2)

    barrier = pltpu.get_barrier_semaphore()
    for dy in (-1, 1, 0):

        def greet(dy=dy):
            for j in range(nx - 1, -1, -1):
                for dz in (0,) + z_steps:
                    if (j, dy, dz) != (0, 0, 0):

                        def hail(j=j, dz=dz):
                            pl.semaphore_signal(barrier, inc=1, device_id=device(j, dy, dz), device_id_type=MESH)

                        guarded(0, dz, hail)

        guarded(dy, 0, greet)

    sections = {}
    for name, (row, height, width) in parts_of.items():
        sections[name] = table_ref.at[pl.ds(row, height), pl.ds(0, width)]
    load_disp = pltpu.make_async_copy(disp_hbm, disp_ref, load_sem.at[0])
    load_table = pltpu.make_async_copy(table_hbm.at[me[0]], table_ref, load_sem.at[1])
    span = sizex // chunks
    for c in range(chunks):
        for i, hbm in enumerate((ref_hbm, def_hbm)):
            pltpu.make_async_copy(
                hbm.at[pl.ds(c * span, span)], image_ref.at[i, pl.ds(c * span, span)], image_sem.at[c]
            ).start()
    load_disp.start()
    load_table.start()

    def clear(test, *parts):
        @pl.when(test)
        def _():
            for part in parts:
                part[...] = jnp.zeros(part.shape, part.dtype)

    low_y, high_y = me[1] == 0, me[1] == ny - 1
    low_z, high_z = me[2] == 0, me[2] == nz - 1
    clear(low_y, yhalo.at[0], mail.at[0], rims.at[:, 0])
    clear(high_y, yhalo.at[1], mail.at[2], rims.at[:, 2])
    clear(low_z, rims.at[0])
    clear(high_z, rims.at[1])
    if nz > 2:
        clear(low_z, zhalo.at[0])
        clear(high_z, zhalo.at[1])
    foot[...] = jnp.zeros(foot.shape, jnp.float32)

    reach = [
        1 + (at > 0).astype(jnp.int32) + (at < count - 1).astype(jnp.int32)
        for at, count in zip(me, counts)
    ]
    expect = nx * reach[1] * (2 if nz == 2 else reach[2]) - 1

    def remote(src, dst, send, recv, to):
        return pltpu.make_async_remote_copy(
            src_ref=src, dst_ref=dst, send_sem=send, recv_sem=recv, device_id=to, device_id_type=MESH
        )

    body = pl.ds(0, cells_z)
    quarter = cells_z // 2
    part_rows = {0: (0, 5 * quarter), 1: (0, 3 * quarter), -1: (2 * quarter, 3 * quarter)}
    part_rims = {0: (0, 4), 1: (0, 3), -1: (1, 3)}

    def mail_copy(j, dy):
        where = pl.ds(*part_rows[dy])
        return remote(
            mail.at[1, me[0], where], mail.at[1 - dy, me[0], where],
            mail_send.at[1 + dy, 0], mail_recv.at[1 - dy, 0], device(j, dy, 0),
        )

    def rim_copy(j, dy, dz):
        side, where = side_out(dz), pl.ds(*part_rims[dy])
        return remote(
            own_rim.at[side, where], rims.at[side, 1 - dy, me[0], where],
            mail_send.at[1 + dy, lane_of(dz)], mail_recv.at[1 - dy, lane_of(dz)], device(j, dy, dz),
        )

    unit = 128 * 4
    plane_bytes = {"x": 2 * sizey * sizez, "y": 2 * sizex * sizez, "z": 2 * sizex * sizey * sizez}

    def settle(dy, sent):
        def one(dz_of, bytes_of):
            lane = lane_of(dz_of if sent else -dz_of)
            ref = grad_y.at[pl.ds(0, bytes_of // unit)]
            copy = remote(ref, ref, mail_send.at[1 + dy, lane], mail_recv.at[1 + dy, lane], device(1, 0, 0))
            copy.wait_send() if sent else copy.wait_recv()

        flat = (nx if dy else nx - 1) * part_rows[dy][1] * unit
        rim = nx * part_rims[dy][1] * unit
        if dy == 0:
            flat += 2 * plane_bytes["x"]
            rim += plane_bytes["z"] if sent else 0
        elif sent:
            flat += plane_bytes["y"]
        if nz == 2:
            guarded(dy, 0, lambda: one(0, flat + rim))
        else:

            def act():
                one(0, flat)
                for dz in z_steps:
                    guarded(0, dz, lambda dz=dz: one(dz, rim))

            guarded(dy, 0, act)

    def bin_cell(cell, carry):
        at = pl.multiple_of(cell * 8, 8)
        total = [None, None]
        for i in range(BIN):
            x = cell * BIN + i
            slabs = (ref_ref[x].astype(jnp.float32), def_ref[x].astype(jnp.float32))
            yrows[0, pl.ds(x, 1), :] = slabs[0][:1]
            yrows[1, pl.ds(x, 1), :] = slabs[0][sizey - 1 :]
            total = [s if t is None else t + s for t, s in zip(total, slabs)]
        for image in range(2):
            for y in range(2):
                binned[2 * image + y, pl.ds(at, 8), :] = total[image][8 * y : 8 * y + 8]
        return carry

    def bin_chunk(c):
        both = image_ref.at[:, pl.ds(c * span, span)]
        pltpu.make_async_copy(both, both, image_sem.at[c]).wait()
        each = cells_x // chunks
        lax.fori_loop(c * each, (c + 1) * each, bin_cell, 0)

    for c in range(chunks):
        bin_chunk(c)

    load_table.wait()
    for q, spots in enumerate(((0, 1), (2, 3), (4, 6), (5, 7))):
        line = binned[q, pl.ds(0, cells_x, stride=8), :]
        for s in range(1, 8):
            line = line + binned[q, pl.ds(s, cells_x, stride=8), :]
        for i, part in enumerate(pieces(line, 3)):
            for spot in spots:
                at = (lax.rem(turn + spot, groups) + spot // groups * groups) * cells_x
                stack[pl.ds(pl.multiple_of(at, cells_x), cells_x), pl.ds(i * sizez, sizez)] = part
    sums = across_lanes(sections["bin"][...], stack[...])
    load_disp.wait()
    lane = lax.broadcasted_iota(jnp.int32, (cells_z, 128), 1)
    held = lax.rem(lane // cells_x + groups - turn, groups)
    empty = jnp.zeros((cells_z, cells_x), jnp.float32)

    def turned_tile(row):
        return pltpu.roll(jnp.concatenate(row, axis=1), turn * cells_x, 1)

    upper = turned_tile([disp_ref[0, 1], disp_ref[1, 1], disp_ref[2, 1], empty])
    lower = turned_tile([disp_ref[1, 0], disp_ref[2, 0], empty, disp_ref[0, 0]])
    upper = jnp.where(held == 3, sums[:, 128:], upper)
    lower = jnp.where(held == 2, sums[:, 128:], lower)
    middle = jnp.where(held[:quarter] % 2 == 0, sums[:quarter, :128], sums[quarter:, :128])
    mail[1, me[0], pl.ds(0, cells_z)] = upper
    mail[1, me[0], pl.ds(cells_z, quarter)] = middle
    mail[1, me[0], pl.ds(cells_z + quarter, cells_z)] = lower
    for side, rows_out in (
        (0, (upper[cells_z - 1 :], middle[quarter - 2 : quarter - 1], middle[quarter - 1 :], lower[cells_z - 1 :])),
        (1, (upper[:1], middle[:1], middle[1:2], lower[:1])),
    ):
        for i, row_out in enumerate(rows_out):
            own_rim[side, i] = row_out
    pl.semaphore_wait(barrier, expect)
    for dy in (-1, 1, 0):

        def act(dy=dy):
            for j in list(range(nx - 1, 0, -1)) + ([0] if dy else []):
                mail_copy(j, dy).start()
            for j in range(nx - 1, -1, -1):
                for dz in z_steps:
                    guarded(0, dz, lambda j=j, dz=dz: rim_copy(j, dy, dz).start())

        guarded(dy, 0, act)

    def x_copy(step):
        side = 0 if step > 0 else 1
        return remote(
            ref_ref.at[pl.ds(sizex - 1 if step > 0 else 0, 1)], xhalo.at[pl.ds(side, 1)],
            mail_send.at[1, 0], mail_recv.at[1, 0], device(1 if step > 0 else nx - 1, 0, 0),
        )

    def y_copy(step):
        side = 1 if step > 0 else 0
        return remote(
            ysend.at[side], yhalo.at[1 - side], mail_send.at[1 + step, 0], y_recv.at[1 - side], device(0, step, 0)
        )

    def z_copy(dz):
        i = 0 if dz > 0 else 1
        return remote(ref_ref, zhalo.at[i], mail_send.at[1, lane_of(dz)], z_recv.at[i], device(0, 0, dz))

    ysend[...] = yrows[...].astype(half)
    for step in (-1, 1):
        guarded(step, 0, lambda step=step: y_copy(step).start())
        x_copy(step).start()
    for dz in z_steps:
        guarded(0, dz, lambda dz=dz: z_copy(dz).start())

    def prepare(cell, carry):
        start = pl.multiple_of(cell * BIN, BIN)
        first = jnp.maximum(start - 1, 0)
        last = jnp.minimum(start + BIN, sizex - 1)
        slabs = [ref_ref[first].astype(jnp.float32)]
        slabs += [ref_ref[start + i].astype(jnp.float32) for i in range(BIN)]
        slabs += [ref_ref[last].astype(jnp.float32)]
        for i in range(BIN):
            base[start + i] = def_ref[start + i].astype(jnp.float32) - slabs[i + 1]
            grad_x[start + i] = slabs[i + 2] - slabs[i]
        return carry

    lax.fori_loop(0, cells_x, prepare, 0)

    slab_row = lax.broadcasted_iota(jnp.int32, (sizey, sizez), 0)

    def slope_y(cell, carry):
        start = pl.multiple_of(cell * BIN, BIN)
        for i in range(BIN):
            slab = ref_ref[start + i].astype(jnp.float32)
            above = jnp.where(slab_row == sizey - 1, 0.0, pltpu.roll(slab, sizey - 1, 0))
            below = jnp.where(slab_row == 0, 0.0, pltpu.roll(slab, 1, 0))
            grad_y[pl.ds(pl.multiple_of((start + i) * sizey, sizey), sizey)] = above - below
        return carry

    lax.fori_loop(0, cells_x, slope_y, 0, unroll=2)

    for dz in z_steps:
        guarded(0, dz, lambda dz=dz: z_copy(-dz if nz > 2 else dz).wait_recv())

    row = lax.broadcasted_iota(jnp.int32, (sizez, sizez), 0)
    column = lax.broadcasted_iota(jnp.int32, (sizez, sizez), 1)
    inner = jnp.where(row == column + 1, 1.0, 0.0) - jnp.where(row + 1 == column, 1.0, 0.0)
    from_low = jnp.where(
        jnp.logical_and(jnp.logical_and(row == sizez - 1, column == 0), me[2] > 0), -1.0, 0.0
    )
    from_high = jnp.where(
        jnp.logical_and(jnp.logical_and(row == 0, column == sizez - 1), me[2] < nz - 1), 1.0, 0.0
    )
    outer = [from_low + from_high] if nz == 2 else [from_low, from_high]
    across = jnp.concatenate([inner] + outer, axis=0).astype(half)

    def slope_z(cell, carry):
        start = pl.multiple_of(cell * BIN, BIN)
        sideways = [ref_ref[pl.ds(start, BIN)].reshape(BIN * sizey, sizez)]
        sideways += [zhalo[i, pl.ds(start, BIN)].reshape(BIN * sizey, sizez) for i in range(len(z_steps))]
        slope = jnp.dot(jnp.concatenate(sideways, axis=1), across, preferred_element_type=jnp.float32)
        grad_z[pl.ds(start, BIN)] = slope.reshape(BIN, sizey, sizez)
        return carry

    lax.fori_loop(0, cells_x, slope_z, 0, unroll=8)

    def gather(tiles, q):
        height = tiles[0].shape[0]
        group = lax.broadcasted_iota(jnp.int32, (height, 128), 1) // cells_x
        out = []
        for t in range(nx // groups):
            value = tiles[t * groups + (-q) % groups]
            for g in range(1, groups):
                value = jnp.where(group == g, tiles[t * groups + (g - q) % groups], value)
            out.append(pltpu.roll(value, (groups - q) * cells_x, 1) if q else value)
        return out[0] if len(out) == 1 else jnp.concatenate(out, axis=1)

    blank = jnp.zeros((SLOT - deep, across_x), jnp.float32)

    def split_store(target, k, y, value, count):
        padded = jnp.concatenate([value, blank], axis=0)
        for i, part in enumerate(pieces(padded, count)):
            target[pl.ds((4 * k + y) * SLOT, SLOT), pl.ds(i * across_x, across_x)] = part

    bottom = deep - cells_z
    foot_row = lax.broadcasted_iota(jnp.int32, (bottom, across_x), 0)

    def unpack(slot):
        for i in range(nx):
            if slot < 2:
                foot[slot, i, 0, pl.ds(0, 1)] = rims[1, slot, i, 0]
                foot[slot, i, 0, pl.ds(bottom - 1, 1)] = rims[0, slot, i, 0]
            for r in range(2):
                foot[slot, i, 1, pl.ds(r, 1)] = rims[1, slot, i, 1 + r]
                foot[slot, i, 1, pl.ds(bottom - 2 + r, 1)] = rims[0, slot, i, 1 + r]
            if slot > 0:
                foot[slot, i, 2, pl.ds(0, 1)] = rims[1, slot, i, 3]
                foot[slot, i, 2, pl.ds(bottom - 1, 1)] = rims[0, slot, i, 3]
        halves = [mail[slot, i, pl.ds(cells_z, quarter)] for i in range(nx)]
        feet = [foot[slot, i, 1] for i in range(nx)]
        for y in range(2):
            cline[2 * slot + y] = jnp.concatenate(
                [
                    gather(halves, 2 * y), gather(halves, 2 * y + 1),
                    jnp.where(foot_row < bottom // 2, gather(feet, 2 * y), gather(feet, 2 * y + 1)),
                ],
                axis=0,
            )
        for y, first, which, order in ((1, 0, 0, (0, 1, 2, 3)), (0, 3 * quarter, 2, (3, 0, 1, 2))):
            line = {(0, 1): 0, (1, 0): 1, (1, 1): 2, (2, 0): 3}.get((slot, y))
            if line is None:
                continue
            tiles = [
                jnp.concatenate([mail[slot, i, pl.ds(first, cells_z)], foot[slot, i, which]], axis=0)
                for i in range(nx)
            ]
            for k in range(3):
                value = gather(tiles, order[k])
                dline[k, line] = value
                split_store(dsplit, k, line, value, 3)
            fline[line] = gather(tiles, order[3])

    settle(0, False)
    grad_x[0] = ref_ref[1].astype(jnp.float32) - jnp.where(me[0] > 0, xhalo[0].astype(jnp.float32), 0.0)
    grad_x[sizex - 1] = (
        jnp.where(me[0] < nx - 1, xhalo[1].astype(jnp.float32), 0.0) - ref_ref[sizex - 2].astype(jnp.float32)
    )
    unpack(1)
    settle(-1, False)
    settle(1, False)
    unpack(0)
    unpack(2)
    kept = across_lanes(sections["pick"][...], dsplit[...])
    lane = lax.broadcasted_iota(jnp.int32, (deep, across_x), 1)
    for y in range(4):
        c = cline[y + 1]
        slopes = [
            (
                jnp.where(lane == across_x - 1, 0.0, pltpu.roll(c, across_x - 1, 1))
                - jnp.where(lane == 0, 0.0, pltpu.roll(c, 1, 1))
            ) * 0.5,
            (cline[y + 2] - cline[y]) * 0.5,
            (pltpu.roll(c, deep - 1, 0) - pltpu.roll(c, 1, 0)) * 0.5,
        ]
        mismatch = fline[y] - c - (
            slopes[0] * dline[0, y] + slopes[1] * dline[1, y] + slopes[2] * dline[2, y]
        )
        for k in range(3):
            split_store(rsplit, k, y, slopes[k] * mismatch, 2)
    step = across_lanes(sections["solve"][...], rsplit[...])
    new = kept + (step[:rows] + step[rows:])
    new_ref[...] = new
    parts = [
        jnp.concatenate(pieces(new[:, 4 * SLOT * k : 4 * SLOT * (k + 1)], 2), axis=1) for k in range(3)
    ]
    along = jnp.dot(jnp.concatenate(parts, axis=0), sections["prolong"][...], preferred_element_type=jnp.float32)
    for k in range(3):
        for s in range(4):
            lines[k, s] = along[rows * k : rows * (k + 1), sizez * s : sizez * (s + 1)]

    for step in (-1, 1):
        guarded(step, 0, lambda step=step: y_copy(-step).wait_recv())
    for at, side in ((0, 0), (sizey - 1, 1)):
        edge = pl.ds(at, sizex, stride=sizey)
        plane = yhalo[side].astype(jnp.float32)
        grad_y[edge, :] = grad_y[edge, :] + plane if side else grad_y[edge, :] - plane
    for dy in (0, -1, 1):
        settle(dy, True)


def combine(
    chunks,
    new_in, lines, base, grad_x, grad_y, grad_z,
    new_hbm, out_hbm,
    out, turned, new_sem, out_sem,
):
    sizex, sizey, sizez = base.shape
    cells_x = sizex // BIN
    span = sizex // chunks
    keep_new = pltpu.make_async_copy(turned, new_hbm, new_sem.at[0])
    cells_z = sizez // BIN
    before_row = new_in.shape[0] - 1

    third = lax.broadcasted_iota(jnp.int32, (8, sizez), 0).astype(jnp.float32)
    offset_y = (third + 0.5) / 8.0 - 0.5
    weight_low = jnp.maximum(-offset_y, 0.0)
    weight_high = jnp.maximum(offset_y, 0.0)
    weight_mid = 1.0 - jnp.abs(offset_y)

    def plane(at):
        planes = []
        for k in range(3):
            row_of = [lines[k, s, pl.ds(at, 1), :] for s in range(4)]
            planes.append(
                jnp.concatenate(
                    [
                        weight_low * row_of[c] + weight_mid * row_of[c + 1] + weight_high * row_of[c + 2]
                        for c in range(2)
                    ],
                    axis=0,
                )
            )
        return planes

    def residual(cell, carry):
        now, rise = carry
        later = plane(cell + 1)
        climb = [(b - a) * 0.125 for a, b in zip(now, later)]
        start = pl.multiple_of(cell * BIN, BIN)
        for i in range(BIN):
            if i == 0:
                field = [n - 3.5 * r for n, r in zip(now, rise)]
            elif i == BIN // 2:
                field = [n + 0.5 * c for n, c in zip(now, climb)]
            else:
                field = [f + d for f, d in zip(field, rise if i < BIN // 2 else climb)]
            total = base[start + i]
            at_y = pl.ds(pl.multiple_of((start + i) * sizey, sizey), sizey)
            total = total - grad_x[start + i] * field[0]
            total = total - grad_y[at_y] * field[1]
            total = total - grad_z[start + i] * field[2]
            out[start + i] = total.astype(jnp.bfloat16)
        return (later, climb)

    def store(c):
        slabs = pl.ds(c * span, span)
        return pltpu.make_async_copy(out.at[slabs], out_hbm.at[slabs], out_sem.at[c])

    before, now = plane(before_row), plane(0)
    state = (now, [(b - a) * 0.125 for a, b in zip(before, now)])
    for c in range(chunks):
        each = cells_x // chunks
        state = lax.fori_loop(c * each, (c + 1) * each, residual, state)
        store(c).start()
        if c == 0:
            for k in range(3):
                flipped = new_in[:cells_x, 4 * SLOT * k : 4 * SLOT * (k + 1)].T
                for y in range(2):
                    turned[k, y] = flipped[SLOT * (y + 1) : SLOT * (y + 1) + cells_z]
            keep_new.start()
    for c in range(chunks):
        store(c).wait()
    keep_new.wait()


def on_device(counts, ref_image, def_image, displacement):
    nx, ny, nz = counts
    sizex, sizey, sizez = ref_image.shape
    cells_x, cells_z = sizex // BIN, sizez // BIN
    rows, deep, across_x = cells_x + 16, cells_z + 8, nx * cells_x
    solve, pick = solve_tables(nx, cells_x, rows)
    binning, prolong = lane_tables(cells_z, sizez, deep, 4)
    parts_of, at = {}, 0
    for name, part in (("prolong", prolong), ("solve", solve), ("pick", pick), ("bin", binning)):
        parts_of[name] = (at, part.shape[-2], part.shape[-1])
        at += part.shape[-2]
    table = np.zeros((nx, at, max(width for _, _, width in parts_of.values())), half)
    for name, part in (("prolong", prolong), ("solve", solve), ("pick", pick), ("bin", binning)):
        row, height, width = parts_of[name]
        table[:, row : row + height, :width] = part
    lanes = 1 if nz == 2 else 3
    sides = 1 if nz == 2 else 2
    dma = pltpu.SemaphoreType.DMA
    vmem, anywhere = pl.BlockSpec(memory_space=pltpu.VMEM), pl.BlockSpec(memory_space=pl.ANY)
    shape = jax.ShapeDtypeStruct
    image = ref_image.shape
    coarse = jnp.transpose(displacement, (0, 2, 3, 1))
    constants = (table,)
    f32 = jnp.float32
    held = pl.pallas_call(
        functools.partial(exchange, counts, 4, parts_of),
        out_shape=(
            shape((rows, 12 * SLOT), f32),
            shape((3, 4, rows, sizez), f32),
            shape(image, f32),
            shape(image, f32),
            shape((sizex * sizey, sizez), f32),
            shape(image, f32),
        ),
        in_specs=[pl.BlockSpec(memory_space=pltpu.HBM)] * 4,
        out_specs=(vmem,) * 6,
        scratch_shapes=[
            pltpu.VMEM((sides,) + image, half),
            pltpu.VMEM((2,) + image, half),
            pltpu.VMEM(coarse.shape, f32),
            pltpu.VMEM(table.shape[1:], half),
            pltpu.VMEM((4, cells_x * 8, sizez), f32),
            pltpu.VMEM((8 * cells_x, 3 * sizez), half),
            pltpu.VMEM((3, nx, 5 * cells_z // 2, 128), f32),
            pltpu.VMEM((2, 3, nx, 4, 1, 128), f32),
            pltpu.VMEM((2, 4, 1, 128), f32),
            pltpu.VMEM((3, nx, 3, deep - cells_z, 128), f32),
            pltpu.VMEM((3, 4, deep, across_x), f32),
            pltpu.VMEM((6, deep, across_x), f32),
            pltpu.VMEM((4, deep, across_x), f32),
            pltpu.VMEM((12 * SLOT, 3 * across_x), half),
            pltpu.VMEM((12 * SLOT, 2 * across_x), half),
            pltpu.VMEM((2, sizey, sizez), half),
            pltpu.VMEM((2, sizex, sizez), f32),
            pltpu.VMEM((2, sizex, sizez), half),
            pltpu.VMEM((2, sizex, sizez), half),
            dma((2,)), dma((4,)), dma((3, lanes)), dma((3, lanes)), dma((2,)), dma((sides,)),
        ],
        compiler_params=pltpu.CompilerParams(
            collective_id=0, has_side_effects=True, vmem_limit_bytes=24 << 20
        ),
    )(*[pltpu.with_memory_space_constraint(jnp.asarray(x), pltpu.HBM) for x in (ref_image, def_image, coarse) + constants])
    chunks = 4
    new, residual = pl.pallas_call(
        functools.partial(combine, chunks),
        out_shape=(shape(coarse.shape, f32), shape(image, half)),
        in_specs=[vmem] * 6,
        out_specs=(anywhere, anywhere),
        scratch_shapes=[pltpu.VMEM(image, half), pltpu.VMEM(coarse.shape, f32), dma((1,)), dma((chunks,))],
        compiler_params=pltpu.CompilerParams(vmem_limit_bytes=16 << 20),
    )(*held)
    return jnp.transpose(new, (0, 3, 1, 2)), residual


def solution(mesh):
    counts = tuple(mesh.shape[axis] for axis in ("gx", "gy", "gz"))
    return jax.shard_map(
        functools.partial(on_device, counts),
        mesh=mesh,
        in_specs=(P("gx", "gy", "gz"), P("gx", "gy", "gz"), P(None, "gx", "gy", "gz")),
        out_specs=(P(None, "gx", "gy", "gz"), P("gx", "gy", "gz")),
        check_vma=False,
    )
```

time: 15.2 us -> 13.2 us (0.87)
  Pallas kernels: 14.4 us -> 12.5 us
    pallas_call x1, Pallas kernels: 12.5 us -> 10.5 us  [on_device(): pl.pallas_call(functools.partial(exchange, counts, 4, parts_of), out_shap...]
where the time goes in v4:
time: 13.2 us; the launch traced here: 13.1 us
  Pallas kernels  12.5 us (95%)
  between operations  0.64 us (5%)
    pallas_call x1, Pallas kernels, on_device(): pl.pallas_call(functools.partial(exchange, counts, 4, parts_of), out_shap...  10.5 us
    pallas_call x1, Pallas kernels, on_device(): pl.pallas_call(functools.partial(combine, chunks), out_shape=(shape(coars...  1.92 us

profile of v4, /device:TPU:0, one launch (start us, length us, event | category | flops | bytes accessed | tf_op | source)
XLA Modules:
  0.0 13.1 jit_solution(15508555675845955951)
XLA Ops:
  0.6 10.5 %shard_map.59 = (f32[48,384]{1,0:T(8,128)S(1)}, f32[3,4,48,128]{3,2,1,0:T(8,128)S(1)}, f32[256,16,128]{2,1,0:T(8,128)S(1)}, f32[256,16,128]{2,1,0:T(8,128)S(1)},...) custom-call(bf16[256,16,128]{2,1,0:T(8,128)(2,1)} %ref_hbm.1, bf16[256,16,128]{2,1,0:T(8,128)(2,1)} %def_hbm.1, ...), custom_call_target="tpu_custom_call" | custom-call | tf_op jit(solution)/shard_map/pallas_call | solution.py:562
  11.2 1.9 %shard_map.60 = (f32[3,2,16,32]{3,2,1,0:T(8,128)}, bf16[256,16,128]{2,1,0:T(8,128)(2,1)}) custom-call(f32[48,384]{1,0:T(8,128)S(1)} %get-tuple-element.10.new_in, f32[3,4,48,128]{3,2,1,0:T(8,128)S(1)} %get-tuple-element.11.lines, f32[256,16,128]{2,1,0:T(8,128)S(1)} %get-tuple-element.12.base, f32[256,16,128]{2,1,0:T(8,128)S(1)} %get-tuple-element.13.grad_x, ...), custom_call_target="tpu_custom_call" | custom-call | tf_op jit(solution)/shard_map/pallas_call | solution.py:601

commit v5 on v4

--- a/solution.py
+++ b/solution.py
@@ -11,6 +11,7 @@
 stiffness = 64.0
 BIN = 8
 SLOT = 32
+PITCH = 24
 MESH = pl.DeviceIdType.MESH
 half = jnp.bfloat16
 
@@ -27,7 +28,6 @@
         / (2.0 * stiffness * np.sinh(theta))
     )
     solve = np.zeros((devices, 2 * rows, 2 * lines), np.float32)
-    pick = np.zeros((devices, rows, 3 * lines), np.float32)
     for me in range(devices):
         first = me * cells
         for row, x in [(r, first + r) for r in range(cells + 1)] + [(rows - 1, first - 1)]:
@@ -37,8 +37,7 @@
             solve[me, row, :lines] = top
             solve[me, row, lines:] = top
             solve[me, rows + row, :lines] = inverse[x] - top
-            pick[me, row, x::lines] = 1.0
-    return solve.astype(half), pick.astype(half)
+    return solve.astype(half)
 
 
 def lane_tables(cells_z, size_z, deep, slots):
@@ -72,7 +71,7 @@
     ref_hbm, def_hbm, disp_hbm, table_hbm,
     new_ref, lines, base, grad_x, grad_y, grad_z,
     zhalo, image_ref, disp_ref, table_ref,
-    binned, stack, mail, rims, own_rim, foot, dline, cline, fline, dsplit, rsplit,
+    binned, stack, mail, rims, own_rim, foot, dline, cline, fline, kept, rsplit,
     xhalo, yrows, ysend, yhalo,
     load_sem, image_sem, mail_send, mail_recv, y_recv, z_recv,
 ):
@@ -87,9 +86,10 @@
     me = (lax.axis_index("gx"), lax.axis_index("gy"), lax.axis_index("gz"))
     turn = lax.rem(me[0], groups)
 
-    def device(j, dy, dz):
+    def device(j, dy, dz, mirrored=False):
         gz = me[2] + dz if nz > 2 or dz == 0 else 1 - me[2]
-        return {"gx": lax.rem(me[0] + j, nx), "gy": me[1] + dy, "gz": gz}
+        gx = lax.rem(2 * nx - 1 - me[0] - j, nx) if mirrored else lax.rem(me[0] + j, nx)
+        return {"gx": gx, "gy": me[1] + dy, "gz": gz}
 
     def guarded(dy, dz, act):
         tests = []
@@ -108,21 +108,6 @@
 
     def lane_of(dz):
         return 0 if nz == 2 or dz == 0 else (1 if dz > 0 else 2)
-
-    barrier = pltpu.get_barrier_semaphore()
-    for dy in (-1, 1, 0):
-
-        def greet(dy=dy):
-            for j in range(nx - 1, -1, -1):
-                for dz in (0,) + z_steps:
-                    if (j, dy, dz) != (0, 0, 0):
-
-                        def hail(j=j, dz=dz):
-                            pl.semaphore_signal(barrier, inc=1, device_id=device(j, dy, dz), device_id_type=MESH)
-
-                        guarded(0, dz, hail)
-
-        guarded(dy, 0, greet)
 
     sections = {}
     for name, (row, height, width) in parts_of.items():
@@ -135,6 +120,21 @@
             pltpu.make_async_copy(
                 hbm.at[pl.ds(c * span, span)], image_ref.at[i, pl.ds(c * span, span)], image_sem.at[c]
             ).start()
+    barrier = pltpu.get_barrier_semaphore()
+    for dy in (-1, 1, 0):
+
+        def greet(dy=dy):
+            for j in range(nx):
+                for dz in (0,) + z_steps:
+                    if (j, dy, dz) != (0, 0, 0):
+
+                        def hail(j=j, dz=dz):
+                            pl.semaphore_signal(barrier, inc=1, device_id=device(j, dy, dz, dy != 0), device_id_type=MESH)
+
+                        guarded(0, dz, hail)
+
+        guarded(dy, 0, greet)
+
     load_disp.start()
     load_table.start()
 
@@ -154,6 +154,7 @@
         clear(low_z, zhalo.at[0])
         clear(high_z, zhalo.at[1])
     foot[...] = jnp.zeros(foot.shape, jnp.float32)
+    kept[...] = jnp.zeros(kept.shape, jnp.float32)
 
     reach = [
         1 + (at > 0).astype(jnp.int32) + (at < count - 1).astype(jnp.int32)
@@ -175,14 +176,14 @@
         where = pl.ds(*part_rows[dy])
         return remote(
             mail.at[1, me[0], where], mail.at[1 - dy, me[0], where],
-            mail_send.at[1 + dy, 0], mail_recv.at[1 - dy, 0], device(j, dy, 0),
+            mail_send.at[1 + dy, 0], mail_recv.at[1 - dy, 0], device(j, dy, 0, dy != 0),
         )
 
     def rim_copy(j, dy, dz):
         side, where = side_out(dz), pl.ds(*part_rims[dy])
         return remote(
             own_rim.at[side, where], rims.at[side, 1 - dy, me[0], where],
-            mail_send.at[1 + dy, lane_of(dz)], mail_recv.at[1 - dy, lane_of(dz)], device(j, dy, dz),
+            mail_send.at[1 + dy, lane_of(dz)], mail_recv.at[1 - dy, lane_of(dz)], device(j, dy, dz, dy != 0),
         )
 
     unit = 128 * 4
@@ -214,7 +215,6 @@
             guarded(dy, 0, act)
 
     def bin_cell(cell, carry):
-        at = pl.multiple_of(cell * 8, 8)
         total = [None, None]
         for i in range(BIN):
             x = cell * BIN + i
@@ -224,24 +224,23 @@
             total = [s if t is None else t + s for t, s in zip(total, slabs)]
         for image in range(2):
             for y in range(2):
-                binned[2 * image + y, pl.ds(at, 8), :] = total[image][8 * y : 8 * y + 8]
+                binned[2 * image + y, pl.ds(cell, 1), :] = jnp.sum(
+                    total[image][8 * y : 8 * y + 8], axis=0, keepdims=True
+                )
         return carry
 
     def bin_chunk(c):
         both = image_ref.at[:, pl.ds(c * span, span)]
         pltpu.make_async_copy(both, both, image_sem.at[c]).wait()
         each = cells_x // chunks
-        lax.fori_loop(c * each, (c + 1) * each, bin_cell, 0)
+        lax.fori_loop(c * each, (c + 1) * each, bin_cell, 0, unroll=2)
 
     for c in range(chunks):
         bin_chunk(c)
 
     load_table.wait()
     for q, spots in enumerate(((0, 1), (2, 3), (4, 6), (5, 7))):
-        line = binned[q, pl.ds(0, cells_x, stride=8), :]
-        for s in range(1, 8):
-            line = line + binned[q, pl.ds(s, cells_x, stride=8), :]
-        for i, part in enumerate(pieces(line, 3)):
+        for i, part in enumerate(pieces(binned[q], 3)):
             for spot in spots:
                 at = (lax.rem(turn + spot, groups) + spot // groups * groups) * cells_x
                 stack[pl.ds(pl.multiple_of(at, cells_x), cells_x), pl.ds(i * sizez, sizez)] = part
@@ -272,9 +271,9 @@
     for dy in (-1, 1, 0):
 
         def act(dy=dy):
-            for j in list(range(nx - 1, 0, -1)) + ([0] if dy else []):
-                mail_copy(j, dy).start()
-            for j in range(nx - 1, -1, -1):
+            for j in range(nx):
+                if j or dy:
+                    mail_copy(j, dy).start()
                 for dz in z_steps:
                     guarded(0, dz, lambda j=j, dz=dz: rim_copy(j, dy, dz).start())
 
@@ -326,7 +325,7 @@
             slab = ref_ref[start + i].astype(jnp.float32)
             above = jnp.where(slab_row == sizey - 1, 0.0, pltpu.roll(slab, sizey - 1, 0))
             below = jnp.where(slab_row == 0, 0.0, pltpu.roll(slab, 1, 0))
-            grad_y[pl.ds(pl.multiple_of((start + i) * sizey, sizey), sizey)] = above - below
+            grad_y[pl.ds(pl.multiple_of((start + i) * PITCH, 8), sizey)] = above - below
         return carry
 
     lax.fori_loop(0, cells_x, slope_y, 0, unroll=2)
@@ -409,7 +408,7 @@
             for k in range(3):
                 value = gather(tiles, order[k])
                 dline[k, line] = value
-                split_store(dsplit, k, line, value, 3)
+                kept[k, pl.ds(SLOT * line, deep)] = value
             fline[line] = gather(tiles, order[3])
 
     settle(0, False)
@@ -422,7 +421,6 @@
     settle(1, False)
     unpack(0)
     unpack(2)
-    kept = across_lanes(sections["pick"][...], dsplit[...])
     lane = lax.broadcasted_iota(jnp.int32, (deep, across_x), 1)
     for y in range(4):
         c = cline[y + 1]
@@ -439,21 +437,32 @@
         )
         for k in range(3):
             split_store(rsplit, k, y, slopes[k] * mismatch, 2)
-    step = across_lanes(sections["solve"][...], rsplit[...])
-    new = kept + (step[:rows] + step[rows:])
-    new_ref[...] = new
-    parts = [
-        jnp.concatenate(pieces(new[:, 4 * SLOT * k : 4 * SLOT * (k + 1)], 2), axis=1) for k in range(3)
-    ]
-    along = jnp.dot(jnp.concatenate(parts, axis=0), sections["prolong"][...], preferred_element_type=jnp.float32)
+    wide = 4 * SLOT
+    out_row = lax.broadcasted_iota(jnp.int32, (rows, wide), 0)
+    real = jnp.logical_and(
+        jnp.logical_or(out_row != cells_x, me[0] < nx - 1), jnp.logical_or(out_row != rows - 1, me[0] > 0)
+    )
+
+    def shifted(k):
+        near = pltpu.roll(kept[k], across_x - me[0] * cells_x, 1)
+        head, tail = near[:, :128].T, near[:, across_x - 128 :].T
+        return jnp.where(real, jnp.concatenate([head[: rows - 8], tail[120:]], axis=0), 0.0)
+
     for k in range(3):
+        span_k = pl.ds(wide * k, wide)
+        step = across_lanes(sections["solve"][...], rsplit[span_k, :])
+        new = shifted(k) + (step[:rows] + step[rows:])
+        new_ref[:, span_k] = new
+        along = jnp.dot(
+            jnp.concatenate(pieces(new, 2), axis=1), sections["prolong"][...], preferred_element_type=jnp.float32
+        )
         for s in range(4):
-            lines[k, s] = along[rows * k : rows * (k + 1), sizez * s : sizez * (s + 1)]
+            lines[k, s] = along[:, sizez * s : sizez * (s + 1)]
 
     for step in (-1, 1):
         guarded(step, 0, lambda step=step: y_copy(-step).wait_recv())
     for at, side in ((0, 0), (sizey - 1, 1)):
-        edge = pl.ds(at, sizex, stride=sizey)
+        edge = pl.ds(at, sizex, stride=PITCH)
         plane = yhalo[side].astype(jnp.float32)
         grad_y[edge, :] = grad_y[edge, :] + plane if side else grad_y[edge, :] - plane
     for dy in (0, -1, 1):
@@ -507,7 +516,7 @@
             else:
                 field = [f + d for f, d in zip(field, rise if i < BIN // 2 else climb)]
             total = base[start + i]
-            at_y = pl.ds(pl.multiple_of((start + i) * sizey, sizey), sizey)
+            at_y = pl.ds(pl.multiple_of((start + i) * PITCH, 8), sizey)
             total = total - grad_x[start + i] * field[0]
             total = total - grad_y[at_y] * field[1]
             total = total - grad_z[start + i] * field[2]
@@ -522,7 +531,7 @@
     state = (now, [(b - a) * 0.125 for a, b in zip(before, now)])
     for c in range(chunks):
         each = cells_x // chunks
-        state = lax.fori_loop(c * each, (c + 1) * each, residual, state)
+        state = lax.fori_loop(c * each, (c + 1) * each, residual, state, unroll=4)
         store(c).start()
         if c == 0:
             for k in range(3):
@@ -540,14 +549,14 @@
     sizex, sizey, sizez = ref_image.shape
     cells_x, cells_z = sizex // BIN, sizez // BIN
     rows, deep, across_x = cells_x + 16, cells_z + 8, nx * cells_x
-    solve, pick = solve_tables(nx, cells_x, rows)
+    solve = solve_tables(nx, cells_x, rows)
     binning, prolong = lane_tables(cells_z, sizez, deep, 4)
     parts_of, at = {}, 0
-    for name, part in (("prolong", prolong), ("solve", solve), ("pick", pick), ("bin", binning)):
+    for name, part in (("prolong", prolong), ("solve", solve), ("bin", binning)):
         parts_of[name] = (at, part.shape[-2], part.shape[-1])
         at += part.shape[-2]
     table = np.zeros((nx, at, max(width for _, _, width in parts_of.values())), half)
-    for name, part in (("prolong", prolong), ("solve", solve), ("pick", pick), ("bin", binning)):
+    for name, part in (("prolong", prolong), ("solve", solve), ("bin", binning)):
         row, height, width = parts_of[name]
         table[:, row : row + height, :width] = part
     lanes = 1 if nz == 2 else 3
@@ -566,7 +575,7 @@
             shape((3, 4, rows, sizez), f32),
             shape(image, f32),
             shape(image, f32),
-            shape((sizex * sizey, sizez), f32),
+            shape((sizex * PITCH, sizez), f32),
             shape(image, f32),
         ),
         in_specs=[pl.BlockSpec(memory_space=pltpu.HBM)] * 4,
@@ -576,7 +585,7 @@
             pltpu.VMEM((2,) + image, half),
             pltpu.VMEM(coarse.shape, f32),
             pltpu.VMEM(table.shape[1:], half),
-            pltpu.VMEM((4, cells_x * 8, sizez), f32),
+            pltpu.VMEM((4, cells_x, sizez), f32),
             pltpu.VMEM((8 * cells_x, 3 * sizez), half),
             pltpu.VMEM((3, nx, 5 * cells_z // 2, 128), f32),
             pltpu.VMEM((2, 3, nx, 4, 1, 128), f32),
@@ -585,7 +594,7 @@
             pltpu.VMEM((3, 4, deep, across_x), f32),
             pltpu.VMEM((6, deep, across_x), f32),
             pltpu.VMEM((4, deep, across_x), f32),
-            pltpu.VMEM((12 * SLOT, 3 * across_x), half),
+            pltpu.VMEM((3, 4 * SLOT, across_x), f32),
             pltpu.VMEM((12 * SLOT, 2 * across_x), half),
             pltpu.VMEM((2, sizey, sizez), half),
             pltpu.VMEM((2, sizex, sizez), f32),
@@ -597,7 +606,7 @@
             collective_id=0, has_side_effects=True, vmem_limit_bytes=24 << 20
         ),
     )(*[pltpu.with_memory_space_constraint(jnp.asarray(x), pltpu.HBM) for x in (ref_image, def_image, coarse) + constants])
-    chunks = 4
+    chunks = 8
     new, residual = pl.pallas_call(
         functools.partial(combine, chunks),
         out_shape=(shape(coarse.shape, f32), shape(image, half)),

time: 13.2 us -> 12.8 us (0.970)
  Pallas kernels: 12.5 us -> 12 us
    pallas_call x1, Pallas kernels: 1.92 us -> 1.64 us  [on_device(): pl.pallas_call(functools.partial(combine, chunks), out_shape=(shape(coars...]
    pallas_call x1, Pallas kernels: 10.5 us -> 10.3 us  [on_device(): pl.pallas_call(functools.partial(exchange, counts, 4, parts_of), out_shap...]
where the time goes in v5:
time: 12.8 us; the launch traced here: 12.6 us
  Pallas kernels  12 us (94%)
  between operations  0.64 us (5%)
    pallas_call x1, Pallas kernels, on_device(): pl.pallas_call(functools.partial(exchange, counts, 4, parts_of), out_shap...  10.3 us
    pallas_call x1, Pallas kernels, on_device(): pl.pallas_call(functools.partial(combine, chunks), out_shape=(shape(coars...  1.64 us

profile of v5, /device:TPU:0, one launch (start us, length us, event | category | flops | bytes accessed | tf_op | source)
XLA Modules:
  0.0 12.6 jit_solution(8294299419416667659)
XLA Ops:
  0.6 10.3 %shard_map.59 = (f32[48,384]{1,0:T(8,128)S(1)}, f32[3,4,48,128]{3,2,1,0:T(8,128)S(1)}, f32[256,16,128]{2,1,0:T(8,128)S(1)}, f32[256,16,128]{2,1,0:T(8,128)S(1)},...) custom-call(bf16[256,16,128]{2,1,0:T(8,128)(2,1)} %ref_hbm.1, bf16[256,16,128]{2,1,0:T(8,128)(2,1)} %def_hbm.1, ...), custom_call_target="tpu_custom_call" | custom-call | tf_op jit(solution)/shard_map/pallas_call | solution.py:571
  11.0 1.6 %shard_map.60 = (f32[3,2,16,32]{3,2,1,0:T(8,128)}, bf16[256,16,128]{2,1,0:T(8,128)(2,1)}) custom-call(f32[48,384]{1,0:T(8,128)S(1)} %get-tuple-element.10.new_in, f32[3,4,48,128]{3,2,1,0:T(8,128)S(1)} %get-tuple-element.11.lines, f32[256,16,128]{2,1,0:T(8,128)S(1)} %get-tuple-element.12.base, f32[256,16,128]{2,1,0:T(8,128)S(1)} %get-tuple-element.13.grad_x, ...), custom_call_target="tpu_custom_call" | custom-call | tf_op jit(solution)/shard_map/pallas_call | solution.py:610

commit v6 on v5

--- a/solution.py
+++ b/solution.py
@@ -27,6 +27,7 @@
         np.exp(a + b - c) * (1 - np.exp(-2 * a)) * (1 - np.exp(-2 * b)) / (1 - np.exp(-2 * c))
         / (2.0 * stiffness * np.sinh(theta))
     )
+    pick = np.zeros((devices, rows, 2 * lines), np.float32)
     solve = np.zeros((devices, 2 * rows, 2 * lines), np.float32)
     for me in range(devices):
         first = me * cells
@@ -37,7 +38,8 @@
             solve[me, row, :lines] = top
             solve[me, row, lines:] = top
             solve[me, rows + row, :lines] = inverse[x] - top
-    return solve.astype(half)
+            pick[me, row, x::lines] = 1.0
+    return solve.astype(half), pick.astype(half)
 
 
 def lane_tables(cells_z, size_z, deep, slots):
@@ -69,9 +71,9 @@
 def exchange(
     counts, chunks, parts_of,
     ref_hbm, def_hbm, disp_hbm, table_hbm,
-    new_ref, lines, base, grad_x, grad_y, grad_z,
-    zhalo, image_ref, disp_ref, table_ref,
-    binned, stack, mail, rims, own_rim, foot, dline, cline, fline, kept, rsplit,
+    new_ref, planes, base, grad_x, grad_y, grad_z,
+    zhalo, lines, image_ref, disp_ref, table_ref,
+    binned, stack, mail, rims, own_rim, foot, dline, cline, fline, sline, kept, rsplit,
     xhalo, yrows, ysend, yhalo,
     load_sem, image_sem, mail_send, mail_recv, y_recv, z_recv,
 ):
@@ -154,7 +156,6 @@
         clear(low_z, zhalo.at[0])
         clear(high_z, zhalo.at[1])
     foot[...] = jnp.zeros(foot.shape, jnp.float32)
-    kept[...] = jnp.zeros(kept.shape, jnp.float32)
 
     reach = [
         1 + (at > 0).astype(jnp.int32) + (at < count - 1).astype(jnp.int32)
@@ -176,43 +177,69 @@
         where = pl.ds(*part_rows[dy])
         return remote(
             mail.at[1, me[0], where], mail.at[1 - dy, me[0], where],
-            mail_send.at[1 + dy, 0], mail_recv.at[1 - dy, 0], device(j, dy, 0, dy != 0),
+            mail_send.at[0], mail_recv.at[abs(dy), 0], device(j, dy, 0, dy != 0),
         )
 
     def rim_copy(j, dy, dz):
         side, where = side_out(dz), pl.ds(*part_rims[dy])
         return remote(
             own_rim.at[side, where], rims.at[side, 1 - dy, me[0], where],
-            mail_send.at[1 + dy, lane_of(dz)], mail_recv.at[1 - dy, lane_of(dz)], device(j, dy, dz, dy != 0),
+            mail_send.at[lane_of(dz)], mail_recv.at[abs(dy), lane_of(dz)], device(j, dy, dz, dy != 0),
         )
 
     unit = 128 * 4
     plane_bytes = {"x": 2 * sizey * sizez, "y": 2 * sizex * sizez, "z": 2 * sizex * sizey * sizez}
 
-    def settle(dy, sent):
-        def one(dz_of, bytes_of):
-            lane = lane_of(dz_of if sent else -dz_of)
-            ref = grad_y.at[pl.ds(0, bytes_of // unit)]
-            copy = remote(ref, ref, mail_send.at[1 + dy, lane], mail_recv.at[1 + dy, lane], device(1, 0, 0))
-            copy.wait_send() if sent else copy.wait_recv()
-
-        flat = (nx if dy else nx - 1) * part_rows[dy][1] * unit
-        rim = nx * part_rims[dy][1] * unit
-        if dy == 0:
-            flat += 2 * plane_bytes["x"]
-            rim += plane_bytes["z"] if sent else 0
-        elif sent:
-            flat += plane_bytes["y"]
+    def drain(bytes_of, send, recv, sent):
+        ref = grad_y.at[pl.ds(0, bytes_of // unit)]
+        copy = remote(ref, ref, send, recv, device(1, 0, 0))
+        copy.wait_send() if sent else copy.wait_recv()
+
+    inner_y = jnp.logical_and(me[1] > 0, me[1] < ny - 1)
+
+    def sides(act):
+        pl.when(inner_y)(lambda: act(2))
+        pl.when(jnp.logical_not(inner_y))(lambda: act(1))
+
+    def near_bytes(rim):
+        return nx * part_rims[0][1] * unit if rim else (nx - 1) * part_rows[0][1] * unit + 2 * plane_bytes["x"]
+
+    def far_bytes(rim):
+        return nx * (part_rims if rim else part_rows)[1][1] * unit
+
+    def settle_near():
         if nz == 2:
-            guarded(dy, 0, lambda: one(0, flat + rim))
+            drain(near_bytes(False) + near_bytes(True), mail_send.at[0], mail_recv.at[0, 0], False)
         else:
-
-            def act():
-                one(0, flat)
+            drain(near_bytes(False), mail_send.at[0], mail_recv.at[0, 0], False)
+            for dz in z_steps:
+                guarded(0, dz, lambda dz=dz: drain(near_bytes(True), mail_send.at[0], mail_recv.at[0, lane_of(-dz)], False))
+
+    def settle_far():
+        def act(count):
+            if nz == 2:
+                drain(count * (far_bytes(False) + far_bytes(True)), mail_send.at[0], mail_recv.at[1, 0], False)
+            else:
+                drain(count * far_bytes(False), mail_send.at[0], mail_recv.at[1, 0], False)
                 for dz in z_steps:
-                    guarded(0, dz, lambda dz=dz: one(dz, rim))
-
-            guarded(dy, 0, act)
+                    guarded(
+                        0, dz, lambda dz=dz: drain(count * far_bytes(True), mail_send.at[0], mail_recv.at[1, lane_of(-dz)], False)
+                    )
+
+        sides(act)
+
+    def settle_sent():
+        def act(count):
+            flat = near_bytes(False) + count * (far_bytes(False) + plane_bytes["y"])
+            rim = near_bytes(True) + count * far_bytes(True) + plane_bytes["z"]
+            if nz == 2:
+                drain(flat + rim, mail_send.at[0], mail_recv.at[0, 0], True)
+            else:
+                drain(flat, mail_send.at[0], mail_recv.at[0, 0], True)
+                for dz in z_steps:
+                    guarded(0, dz, lambda dz=dz: drain(rim, mail_send.at[lane_of(dz)], mail_recv.at[0, 0], True))
+
+        sides(act)
 
     def bin_cell(cell, carry):
         total = [None, None]
@@ -267,6 +294,7 @@
     ):
         for i, row_out in enumerate(rows_out):
             own_rim[side, i] = row_out
+    ysend[...] = yrows[...].astype(half)
     pl.semaphore_wait(barrier, expect)
     for dy in (-1, 1, 0):
 
@@ -283,20 +311,19 @@
         side = 0 if step > 0 else 1
         return remote(
             ref_ref.at[pl.ds(sizex - 1 if step > 0 else 0, 1)], xhalo.at[pl.ds(side, 1)],
-            mail_send.at[1, 0], mail_recv.at[1, 0], device(1 if step > 0 else nx - 1, 0, 0),
+            mail_send.at[0], mail_recv.at[0, 0], device(1 if step > 0 else nx - 1, 0, 0),
         )
 
     def y_copy(step):
         side = 1 if step > 0 else 0
         return remote(
-            ysend.at[side], yhalo.at[1 - side], mail_send.at[1 + step, 0], y_recv.at[1 - side], device(0, step, 0)
+            ysend.at[side], yhalo.at[1 - side], mail_send.at[0], y_recv.at[0], device(0, step, 0)
         )
 
     def z_copy(dz):
         i = 0 if dz > 0 else 1
-        return remote(ref_ref, zhalo.at[i], mail_send.at[1, lane_of(dz)], z_recv.at[i], device(0, 0, dz))
-
-    ysend[...] = yrows[...].astype(half)
+        return remote(ref_ref, zhalo.at[i], mail_send.at[lane_of(dz)], z_recv.at[i], device(0, 0, dz))
+
     for step in (-1, 1):
         guarded(step, 0, lambda step=step: y_copy(step).start())
         x_copy(step).start()
@@ -355,7 +382,7 @@
 
     lax.fori_loop(0, cells_x, slope_z, 0, unroll=8)
 
-    def gather(tiles, q):
+    def gather(tiles, q, shift=0):
         height = tiles[0].shape[0]
         group = lax.broadcasted_iota(jnp.int32, (height, 128), 1) // cells_x
         out = []
@@ -363,8 +390,12 @@
             value = tiles[t * groups + (-q) % groups]
             for g in range(1, groups):
                 value = jnp.where(group == g, tiles[t * groups + (g - q) % groups], value)
-            out.append(pltpu.roll(value, (groups - q) * cells_x, 1) if q else value)
-        return out[0] if len(out) == 1 else jnp.concatenate(out, axis=1)
+            turn_by = (-q * cells_x - (shift if nx == groups else 0)) % 128
+            out.append(pltpu.roll(value, turn_by, 1) if turn_by else value)
+        if len(out) == 1:
+            return out[0]
+        whole = jnp.concatenate(out, axis=1)
+        return pltpu.roll(whole, -shift % across_x, 1) if shift else whole
 
     blank = jnp.zeros((SLOT - deep, across_x), jnp.float32)
 
@@ -374,6 +405,7 @@
             target[pl.ds((4 * k + y) * SLOT, SLOT), pl.ds(i * across_x, across_x)] = part
 
     bottom = deep - cells_z
+    lane = lax.broadcasted_iota(jnp.int32, (deep, across_x), 1)
     foot_row = lax.broadcasted_iota(jnp.int32, (bottom, across_x), 0)
 
     def unpack(slot):
@@ -389,15 +421,18 @@
                 foot[slot, i, 2, pl.ds(bottom - 1, 1)] = rims[0, slot, i, 3]
         halves = [mail[slot, i, pl.ds(cells_z, quarter)] for i in range(nx)]
         feet = [foot[slot, i, 1] for i in range(nx)]
-        for y in range(2):
-            cline[2 * slot + y] = jnp.concatenate(
+        def sums_of(y, shift):
+            return jnp.concatenate(
                 [
-                    gather(halves, 2 * y), gather(halves, 2 * y + 1),
-                    jnp.where(foot_row < bottom // 2, gather(feet, 2 * y), gather(feet, 2 * y + 1)),
+                    gather(halves, 2 * y, shift), gather(halves, 2 * y + 1, shift),
+                    jnp.where(foot_row < bottom // 2, gather(feet, 2 * y, shift), gather(feet, 2 * y + 1, shift)),
                 ],
                 axis=0,
             )
-        for y, first, which, order in ((1, 0, 0, (0, 1, 2, 3)), (0, 3 * quarter, 2, (3, 0, 1, 2))):
+
+        for y, first, which, order in ((0, 3 * quarter, 2, (3, 0, 1, 2)), (1, 0, 0, (0, 1, 2, 3))):
+            c = sums_of(y, 0)
+            cline[2 * slot + y] = c
             line = {(0, 1): 0, (1, 0): 1, (1, 1): 2, (2, 0): 3}.get((slot, y))
             if line is None:
                 continue
@@ -405,82 +440,46 @@
                 jnp.concatenate([mail[slot, i, pl.ds(first, cells_z)], foot[slot, i, which]], axis=0)
                 for i in range(nx)
             ]
+            moved = [gather(tiles, order[k]) for k in range(3)]
             for k in range(3):
-                value = gather(tiles, order[k])
-                dline[k, line] = value
-                kept[k, pl.ds(SLOT * line, deep)] = value
-            fline[line] = gather(tiles, order[3])
-
-    settle(0, False)
+                split_store(kept, k, line, moved[k], 2)
+            slope_0 = (
+                jnp.where(lane == across_x - 1, 0.0, sums_of(y, 1)) - jnp.where(lane == 0, 0.0, sums_of(y, -1))
+            ) * 0.5
+            slope_2 = (pltpu.roll(c, deep - 1, 0) - pltpu.roll(c, 1, 0)) * 0.5
+            sline[line, 0] = slope_0
+            sline[line, 1] = slope_2
+            dline[0, line] = moved[1]
+            fline[line] = gather(tiles, order[3]) - c - (slope_0 * moved[0] + slope_2 * moved[2])
+
+    settle_near()
     grad_x[0] = ref_ref[1].astype(jnp.float32) - jnp.where(me[0] > 0, xhalo[0].astype(jnp.float32), 0.0)
     grad_x[sizex - 1] = (
         jnp.where(me[0] < nx - 1, xhalo[1].astype(jnp.float32), 0.0) - ref_ref[sizex - 2].astype(jnp.float32)
     )
     unpack(1)
-    settle(-1, False)
-    settle(1, False)
+    settle_far()
     unpack(0)
     unpack(2)
-    lane = lax.broadcasted_iota(jnp.int32, (deep, across_x), 1)
+    picked = [
+        across_lanes(sections["pick"][...], kept[pl.ds(4 * SLOT * k, 4 * SLOT), :]) for k in range(3)
+    ]
     for y in range(4):
-        c = cline[y + 1]
-        slopes = [
-            (
-                jnp.where(lane == across_x - 1, 0.0, pltpu.roll(c, across_x - 1, 1))
-                - jnp.where(lane == 0, 0.0, pltpu.roll(c, 1, 1))
-            ) * 0.5,
-            (cline[y + 2] - cline[y]) * 0.5,
-            (pltpu.roll(c, deep - 1, 0) - pltpu.roll(c, 1, 0)) * 0.5,
-        ]
-        mismatch = fline[y] - c - (
-            slopes[0] * dline[0, y] + slopes[1] * dline[1, y] + slopes[2] * dline[2, y]
-        )
-        for k in range(3):
-            split_store(rsplit, k, y, slopes[k] * mismatch, 2)
+        slope_1 = (cline[y + 2] - cline[y]) * 0.5
+        mismatch = fline[y] - slope_1 * dline[0, y]
+        for k, slope in enumerate((sline[y, 0], slope_1, sline[y, 1])):
+            split_store(rsplit, k, y, slope * mismatch, 2)
     wide = 4 * SLOT
-    out_row = lax.broadcasted_iota(jnp.int32, (rows, wide), 0)
-    real = jnp.logical_and(
-        jnp.logical_or(out_row != cells_x, me[0] < nx - 1), jnp.logical_or(out_row != rows - 1, me[0] > 0)
-    )
-
-    def shifted(k):
-        near = pltpu.roll(kept[k], across_x - me[0] * cells_x, 1)
-        head, tail = near[:, :128].T, near[:, across_x - 128 :].T
-        return jnp.where(real, jnp.concatenate([head[: rows - 8], tail[120:]], axis=0), 0.0)
-
     for k in range(3):
         span_k = pl.ds(wide * k, wide)
         step = across_lanes(sections["solve"][...], rsplit[span_k, :])
-        new = shifted(k) + (step[:rows] + step[rows:])
+        new = picked[k] + (step[:rows] + step[rows:])
         new_ref[:, span_k] = new
         along = jnp.dot(
             jnp.concatenate(pieces(new, 2), axis=1), sections["prolong"][...], preferred_element_type=jnp.float32
         )
         for s in range(4):
             lines[k, s] = along[:, sizez * s : sizez * (s + 1)]
-
-    for step in (-1, 1):
-        guarded(step, 0, lambda step=step: y_copy(-step).wait_recv())
-    for at, side in ((0, 0), (sizey - 1, 1)):
-        edge = pl.ds(at, sizex, stride=PITCH)
-        plane = yhalo[side].astype(jnp.float32)
-        grad_y[edge, :] = grad_y[edge, :] + plane if side else grad_y[edge, :] - plane
-    for dy in (0, -1, 1):
-        settle(dy, True)
-
-
-def combine(
-    chunks,
-    new_in, lines, base, grad_x, grad_y, grad_z,
-    new_hbm, out_hbm,
-    out, turned, new_sem, out_sem,
-):
-    sizex, sizey, sizez = base.shape
-    cells_x = sizex // BIN
-    span = sizex // chunks
-    keep_new = pltpu.make_async_copy(turned, new_hbm, new_sem.at[0])
-    cells_z = sizez // BIN
-    before_row = new_in.shape[0] - 1
 
     third = lax.broadcasted_iota(jnp.int32, (8, sizez), 0).astype(jnp.float32)
     offset_y = (third + 0.5) / 8.0 - 0.5
@@ -503,9 +502,38 @@
             )
         return planes
 
+    def interpolate(cell, carry):
+        for k, value in enumerate(plane(cell)):
+            planes[cell + 1, k] = value
+        return carry
+
+    for k, value in enumerate(plane(rows - 1)):
+        planes[0, k] = value
+    lax.fori_loop(0, cells_x + 1, interpolate, 0, unroll=3)
+
+    sides(lambda count: drain(count * plane_bytes["y"], mail_send.at[0], y_recv.at[0], False))
+    for at, side in ((0, 0), (sizey - 1, 1)):
+        edge = pl.ds(at, sizex, stride=PITCH)
+        plane = yhalo[side].astype(jnp.float32)
+        grad_y[edge, :] = grad_y[edge, :] + plane if side else grad_y[edge, :] - plane
+    settle_sent()
+
+
+def combine(
+    chunks,
+    new_in, planes, base, grad_x, grad_y, grad_z,
+    new_hbm, out_hbm,
+    out, turned, new_sem, out_sem,
+):
+    sizex, sizey, sizez = base.shape
+    cells_x = sizex // BIN
+    span = sizex // chunks
+    keep_new = pltpu.make_async_copy(turned, new_hbm, new_sem.at[0])
+    cells_z = sizez // BIN
+
     def residual(cell, carry):
         now, rise = carry
-        later = plane(cell + 1)
+        later = [planes[cell + 2, k] for k in range(3)]
         climb = [(b - a) * 0.125 for a, b in zip(now, later)]
         start = pl.multiple_of(cell * BIN, BIN)
         for i in range(BIN):
@@ -525,9 +553,9 @@
 
     def store(c):
         slabs = pl.ds(c * span, span)
-        return pltpu.make_async_copy(out.at[slabs], out_hbm.at[slabs], out_sem.at[c])
-
-    before, now = plane(before_row), plane(0)
+        return pltpu.make_async_copy(out.at[slabs], out_hbm.at[slabs], out_sem.at[0])
+
+    before, now = ([planes[i, k] for k in range(3)] for i in range(2))
     state = (now, [(b - a) * 0.125 for a, b in zip(before, now)])
     for c in range(chunks):
         each = cells_x // chunks
@@ -539,8 +567,7 @@
                 for y in range(2):
                     turned[k, y] = flipped[SLOT * (y + 1) : SLOT * (y + 1) + cells_z]
             keep_new.start()
-    for c in range(chunks):
-        store(c).wait()
+    pltpu.make_async_copy(out, out_hbm, out_sem.at[0]).wait()
     keep_new.wait()
 
 
@@ -549,14 +576,14 @@
     sizex, sizey, sizez = ref_image.shape
     cells_x, cells_z = sizex // BIN, sizez // BIN
     rows, deep, across_x = cells_x + 16, cells_z + 8, nx * cells_x
-    solve = solve_tables(nx, cells_x, rows)
+    solve, pick = solve_tables(nx, cells_x, rows)
     binning, prolong = lane_tables(cells_z, sizez, deep, 4)
     parts_of, at = {}, 0
-    for name, part in (("prolong", prolong), ("solve", solve), ("bin", binning)):
+    for name, part in (("prolong", prolong), ("solve", solve), ("pick", pick), ("bin", binning)):
         parts_of[name] = (at, part.shape[-2], part.shape[-1])
         at += part.shape[-2]
     table = np.zeros((nx, at, max(width for _, _, width in parts_of.values())), half)
-    for name, part in (("prolong", prolong), ("solve", solve), ("bin", binning)):
+    for name, part in (("prolong", prolong), ("solve", solve), ("pick", pick), ("bin", binning)):
         row, height, width = parts_of[name]
         table[:, row : row + height, :width] = part
     lanes = 1 if nz == 2 else 3
@@ -572,7 +599,7 @@
         functools.partial(exchange, counts, 4, parts_of),
         out_shape=(
             shape((rows, 12 * SLOT), f32),
-            shape((3, 4, rows, sizez), f32),
+            shape((cells_x + 2, 3, sizey, sizez), f32),
             shape(image, f32),
             shape(image, f32),
             shape((sizex * PITCH, sizez), f32),
@@ -582,6 +609,7 @@
         out_specs=(vmem,) * 6,
         scratch_shapes=[
             pltpu.VMEM((sides,) + image, half),
+            pltpu.VMEM((3, 4, rows, sizez), f32),
             pltpu.VMEM((2,) + image, half),
             pltpu.VMEM(coarse.shape, f32),
             pltpu.VMEM(table.shape[1:], half),
@@ -591,16 +619,17 @@
             pltpu.VMEM((2, 3, nx, 4, 1, 128), f32),
             pltpu.VMEM((2, 4, 1, 128), f32),
             pltpu.VMEM((3, nx, 3, deep - cells_z, 128), f32),
-            pltpu.VMEM((3, 4, deep, across_x), f32),
+            pltpu.VMEM((1, 4, deep, across_x), f32),
             pltpu.VMEM((6, deep, across_x), f32),
             pltpu.VMEM((4, deep, across_x), f32),
-            pltpu.VMEM((3, 4 * SLOT, across_x), f32),
+            pltpu.VMEM((4, 2, deep, across_x), f32),
+            pltpu.VMEM((12 * SLOT, 2 * across_x), half),
             pltpu.VMEM((12 * SLOT, 2 * across_x), half),
             pltpu.VMEM((2, sizey, sizez), half),
             pltpu.VMEM((2, sizex, sizez), f32),
             pltpu.VMEM((2, sizex, sizez), half),
             pltpu.VMEM((2, sizex, sizez), half),
-            dma((2,)), dma((4,)), dma((3, lanes)), dma((3, lanes)), dma((2,)), dma((sides,)),
+            dma((2,)), dma((4,)), dma((lanes,)), dma((2, lanes)), dma((1,)), dma((sides,)),
         ],
         compiler_params=pltpu.CompilerParams(
             collective_id=0, has_side_effects=True, vmem_limit_bytes=24 << 20
@@ -612,7 +641,7 @@
         out_shape=(shape(coarse.shape, f32), shape(image, half)),
         in_specs=[vmem] * 6,
         out_specs=(anywhere, anywhere),
-        scratch_shapes=[pltpu.VMEM(image, half), pltpu.VMEM(coarse.shape, f32), dma((1,)), dma((chunks,))],
+        scratch_shapes=[pltpu.VMEM(image, half), pltpu.VMEM(coarse.shape, f32), dma((1,)), dma((1,))],
         compiler_params=pltpu.CompilerParams(vmem_limit_bytes=16 << 20),
     )(*held)
     return jnp.transpose(new, (0, 3, 1, 2)), residual

time: 12.8 us -> 12.5 us (0.977)
  Pallas kernels: 12 us -> 11.7 us
    pallas_call x1, Pallas kernels: 1.64 us -> 1.45 us  [on_device(): pl.pallas_call(functools.partial(combine, chunks), out_shape=(shape(coars...]
where the time goes in v6:
time: 12.5 us; the launch traced here: 12.4 us
  Pallas kernels  11.7 us (94%)
  between operations  0.64 us (5%)
    pallas_call x1, Pallas kernels, on_device(): pl.pallas_call(functools.partial(exchange, counts, 4, parts_of), out_shap...  10.3 us
    pallas_call x1, Pallas kernels, on_device(): pl.pallas_call(functools.partial(combine, chunks), out_shape=(shape(coars...  1.45 us

profile of v6, /device:TPU:0, one launch (start us, length us, event | category | flops | bytes accessed | tf_op | source)
XLA Modules:
  0.0 12.4 jit_solution(6202100620059074748)
XLA Ops:
  0.6 10.3 %shard_map.59 = (f32[48,384]{1,0:T(8,128)S(1)}, f32[34,3,16,128]{3,2,1,0:T(8,128)S(1)}, f32[256,16,128]{2,1,0:T(8,128)S(1)}, f32[256,16,128]{2,1,0:T(8,128)S(1)}...) custom-call(bf16[256,16,128]{2,1,0:T(8,128)(2,1)} %ref_hbm.1, bf16[256,16,128]{2,1,0:T(8,128)(2,1)} %def_hbm.1, ...), custom_call_target="tpu_custom_call" | custom-call | tf_op jit(solution)/shard_map/pallas_call | solution.py:598
  10.9 1.4 %shard_map.60 = (f32[3,2,16,32]{3,2,1,0:T(8,128)}, bf16[256,16,128]{2,1,0:T(8,128)(2,1)}) custom-call(f32[48,384]{1,0:T(8,128)S(1)} %get-tuple-element.10.new_in, f32[34,3,16,128]{3,2,1,0:T(8,128)S(1)} %get-tuple-element.11.planes, f32[256,16,128]{2,1,0:T(8,128)S(1)} %get-tuple-element.12.base, f32[256,16,128]{2,1,0:T(8,128)S(1)} %get-tuple-element.13.grad_x, ...), custom_call_target="tpu_custom_call" | custom-call | tf_op jit(solution)/shard_map/pallas_call | solution.py:639

commit v7 on v6

--- a/solution.py
+++ b/solution.py
@@ -470,16 +470,17 @@
         for k, slope in enumerate((sline[y, 0], slope_1, sline[y, 1])):
             split_store(rsplit, k, y, slope * mismatch, 2)
     wide = 4 * SLOT
+    parts = []
     for k in range(3):
         span_k = pl.ds(wide * k, wide)
         step = across_lanes(sections["solve"][...], rsplit[span_k, :])
         new = picked[k] + (step[:rows] + step[rows:])
         new_ref[:, span_k] = new
-        along = jnp.dot(
-            jnp.concatenate(pieces(new, 2), axis=1), sections["prolong"][...], preferred_element_type=jnp.float32
-        )
+        parts.append(jnp.concatenate(pieces(new, 2), axis=1))
+    along = jnp.dot(jnp.concatenate(parts, axis=0), sections["prolong"][...], preferred_element_type=jnp.float32)
+    for k in range(3):
         for s in range(4):
-            lines[k, s] = along[:, sizez * s : sizez * (s + 1)]
+            lines[k, s] = along[rows * k : rows * (k + 1), sizez * s : sizez * (s + 1)]
 
     third = lax.broadcasted_iota(jnp.int32, (8, sizez), 0).astype(jnp.float32)
     offset_y = (third + 0.5) / 8.0 - 0.5
@@ -559,7 +560,7 @@
     state = (now, [(b - a) * 0.125 for a, b in zip(before, now)])
     for c in range(chunks):
         each = cells_x // chunks
-        state = lax.fori_loop(c * each, (c + 1) * each, residual, state, unroll=4)
+        state = lax.fori_loop(c * each, (c + 1) * each, residual, state, unroll=2)
         store(c).start()
         if c == 0:
             for k in range(3):
@@ -635,7 +636,7 @@
             collective_id=0, has_side_effects=True, vmem_limit_bytes=24 << 20
         ),
     )(*[pltpu.with_memory_space_constraint(jnp.asarray(x), pltpu.HBM) for x in (ref_image, def_image, coarse) + constants])
-    chunks = 8
+    chunks = 16
     new, residual = pl.pallas_call(
         functools.partial(combine, chunks),
         out_shape=(shape(coarse.shape, f32), shape(image, half)),

time: 12.5 us -> 12.5 us (level)
  no operation moved by 1% of the time
where the time goes in v7:
time: 12.5 us; the launch traced here: 12.3 us
  Pallas kernels  11.7 us (94%)
  between operations  0.64 us (5%)
    pallas_call x1, Pallas kernels, on_device(): pl.pallas_call(functools.partial(exchange, counts, 4, parts_of), out_shap...  10.3 us
    pallas_call x1, Pallas kernels, on_device(): pl.pallas_call(functools.partial(combine, chunks), out_shape=(shape(coars...  1.42 us

profile of v7, /device:TPU:0, one launch (start us, length us, event | category | flops | bytes accessed | tf_op | source)
XLA Modules:
  0.0 12.3 jit_solution(15119326970487984519)
XLA Ops:
  0.6 10.3 %shard_map.59 = (f32[48,384]{1,0:T(8,128)S(1)}, f32[34,3,16,128]{3,2,1,0:T(8,128)S(1)}, f32[256,16,128]{2,1,0:T(8,128)S(1)}, f32[256,16,128]{2,1,0:T(8,128)S(1)}...) custom-call(bf16[256,16,128]{2,1,0:T(8,128)(2,1)} %ref_hbm.1, bf16[256,16,128]{2,1,0:T(8,128)(2,1)} %def_hbm.1, ...), custom_call_target="tpu_custom_call" | custom-call | tf_op jit(solution)/shard_map/pallas_call | solution.py:599
  10.9 1.4 %shard_map.60 = (f32[3,2,16,32]{3,2,1,0:T(8,128)}, bf16[256,16,128]{2,1,0:T(8,128)(2,1)}) custom-call(f32[48,384]{1,0:T(8,128)S(1)} %get-tuple-element.10.new_in, f32[34,3,16,128]{3,2,1,0:T(8,128)S(1)} %get-tuple-element.11.planes, f32[256,16,128]{2,1,0:T(8,128)S(1)} %get-tuple-element.12.base, f32[256,16,128]{2,1,0:T(8,128)S(1)} %get-tuple-element.13.grad_x, ...), custom_call_target="tpu_custom_call" | custom-call | tf_op jit(solution)/shard_map/pallas_call | solution.py:640

commit v8 on v7

--- a/solution.py
+++ b/solution.py
@@ -327,8 +327,6 @@
     for step in (-1, 1):
         guarded(step, 0, lambda step=step: y_copy(step).start())
         x_copy(step).start()
-    for dz in z_steps:
-        guarded(0, dz, lambda dz=dz: z_copy(dz).start())
 
     def prepare(cell, carry):
         start = pl.multiple_of(cell * BIN, BIN)
@@ -343,6 +341,9 @@
         return carry
 
     lax.fori_loop(0, cells_x, prepare, 0)
+
+    for dz in z_steps:
+        guarded(0, dz, lambda dz=dz: z_copy(dz).start())
 
     slab_row = lax.broadcasted_iota(jnp.int32, (sizey, sizez), 0)
 
@@ -597,7 +598,7 @@
     constants = (table,)
     f32 = jnp.float32
     held = pl.pallas_call(
-        functools.partial(exchange, counts, 4, parts_of),
+        functools.partial(exchange, counts, 2, parts_of),
         out_shape=(
             shape((rows, 12 * SLOT), f32),
             shape((cells_x + 2, 3, sizey, sizez), f32),
@@ -630,7 +631,7 @@
             pltpu.VMEM((2, sizex, sizez), f32),
             pltpu.VMEM((2, sizex, sizez), half),
             pltpu.VMEM((2, sizex, sizez), half),
-            dma((2,)), dma((4,)), dma((lanes,)), dma((2, lanes)), dma((1,)), dma((sides,)),
+            dma((2,)), dma((2,)), dma((lanes,)), dma((2, lanes)), dma((1,)), dma((sides,)),
         ],
         compiler_params=pltpu.CompilerParams(
             collective_id=0, has_side_effects=True, vmem_limit_bytes=24 << 20

time: 12.5 us -> 12.5 us (level)
  no operation moved by 1% of the time
where the time goes in v8:
time: 12.5 us; the launch traced here: 12.3 us
  Pallas kernels  11.7 us (94%)
  between operations  0.64 us (5%)
    pallas_call x1, Pallas kernels, on_device(): pl.pallas_call(functools.partial(exchange, counts, 2, parts_of), out_shap...  10.3 us
    pallas_call x1, Pallas kernels, on_device(): pl.pallas_call(functools.partial(combine, chunks), out_shape=(shape(coars...  1.42 us

profile of v8, /device:TPU:0, one launch (start us, length us, event | category | flops | bytes accessed | tf_op | source)
XLA Modules:
  0.0 12.3 jit_solution(4266361922976804985)
XLA Ops:
  0.6 10.3 %shard_map.59 = (f32[48,384]{1,0:T(8,128)S(1)}, f32[34,3,16,128]{3,2,1,0:T(8,128)S(1)}, f32[256,16,128]{2,1,0:T(8,128)S(1)}, f32[256,16,128]{2,1,0:T(8,128)S(1)}...) custom-call(bf16[256,16,128]{2,1,0:T(8,128)(2,1)} %ref_hbm.1, bf16[256,16,128]{2,1,0:T(8,128)(2,1)} %def_hbm.1, ...), custom_call_target="tpu_custom_call" | custom-call | tf_op jit(solution)/shard_map/pallas_call | solution.py:600
  10.9 1.4 %shard_map.60 = (f32[3,2,16,32]{3,2,1,0:T(8,128)}, bf16[256,16,128]{2,1,0:T(8,128)(2,1)}) custom-call(f32[48,384]{1,0:T(8,128)S(1)} %get-tuple-element.10.new_in, f32[34,3,16,128]{3,2,1,0:T(8,128)S(1)} %get-tuple-element.11.planes, f32[256,16,128]{2,1,0:T(8,128)S(1)} %get-tuple-element.12.base, f32[256,16,128]{2,1,0:T(8,128)S(1)} %get-tuple-element.13.grad_x, ...), custom_call_target="tpu_custom_call" | custom-call | tf_op jit(solution)/shard_map/pallas_call | solution.py:641
